TPU v7x, 256 devices: a whole 4x4x8 slice. The times are simulated.
256 devices in a mesh: seq: 16 (over y, x), width: 16 (over z, core).
Axes of the slice: x: 4, y: 4, z: 8, core: 2. Of those that a mesh axis runs over, the one named last changes fastest.
Arguments:
- leak_rate: float32 [1, 32768, 2048], P(None, 'seq', 'width'), may hold values from 0.2 to 2
- signal_in: bfloat16 [1, 32768, 2048], P(None, 'seq', 'width'), may hold values from -6 to 6
- norm_gain: float32 [2048], P('width'), may hold values from 0.25 to 1.75
Outputs:
- mixed_out: bfloat16 [1, 32768, 2048], P(None, 'seq', 'width')
All inputs are finite; a program needn't handle non-finite values.
Results may differ from a plain program's by a relative error of at most 0.001.
Values sent between devices are 32-bit elements; how exact they have to be, the bound alone decides.
No kernel may reach another device: no remote copies, remote signals or barrier semaphores. Data moves between devices by JAX's collectives and lax.ppermute only.
A program may use at most 64 MiB of HBM per device.

v0:
```python
import jax
import jax.numpy as jnp
from jax import lax
from jax.sharding import PartitionSpec as P


def copy_for_each(x, axis):
    length = lax.axis_size(axis)
    return lax.all_to_all(jnp.broadcast_to(x[None], (length, *x.shape)), axis, 0, 0, tiled=True)


def all_in_one(x, axis):
    leaves = jax.tree.leaves(x)
    turns = sorted(range(len(leaves)), key=lambda k: -leaves[k].size)
    width = (1, *leaves[turns[0]].shape)[-1]
    lines = [
        jnp.pad(leaves[k].reshape(-1), (0, -leaves[k].size % width)).reshape(-1, width)
        for k in turns
    ]
    both, at, found = (copy_for_each(jnp.concatenate(lines), axis), 0, {})
    for k, line in zip(turns, lines):
        section = both[:, at : at + len(line)].reshape(len(both), -1)
        found[k] = section[:, : leaves[k].size].reshape(-1, *leaves[k].shape)
        at += len(line)
    numbers = iter(range(len(leaves)))
    return jax.tree.map(lambda _: found[next(numbers)], x)


def joined_by_halves(pieces, combine):
    while len(jax.tree.leaves(pieces)[0]) > 1:
        pieces = jax.vmap(combine)(
            *(jax.tree.map(lambda part: part[side::2], pieces) for side in (0, 1))
        )
    return jax.tree.map(lambda part: part[0], pieces)


def carried_in(x, axis, combine, identity, reverse):
    length, here = (lax.axis_size(axis), lax.axis_index(axis))
    passed = jnp.arange(length) > here if reverse else jnp.arange(length) < here

    def kept(part, zero, own):
        part = jnp.where(
            passed.reshape(-1, *(1 for _ in own.shape)), part, jnp.asarray(zero, own.dtype)
        )
        return part[::-1] if reverse else part

    pieces = all_in_one(x, axis)
    return joined_by_halves(jax.tree.map(kept, pieces, identity, x), combine)


def taken_together(x, axis):
    everything = copy_for_each(x, axis)
    return jnp.sum(everything, axis=0)


def join_pair(earlier, later):
    return (earlier[0] * later[0], later[0] * earlier[1] + later[1])


def per_device(leak_rate, signal_in, norm_gain):
    total_length = leak_rate.shape[1] * lax.axis_size("seq")
    keep = jnp.exp(-leak_rate / total_length)
    push = signal_in.astype(jnp.float32) * total_length ** (-0.5)
    product, forward = lax.associative_scan(join_pair, (keep, push), axis=1)
    entering_forward = carried_in(
        (product[:, -1], forward[:, -1]),
        "seq",
        join_pair,
        (jnp.ones_like(keep[:, 0]), jnp.zeros_like(push[:, 0])),
        False,
    )
    forward = forward + product * entering_forward[1][:, None]
    product, backward = lax.associative_scan(join_pair, (keep, push), axis=1, reverse=True)
    entering_backward = carried_in(
        (product[:, 0], backward[:, 0]),
        "seq",
        join_pair,
        (jnp.ones_like(keep[:, 0]), jnp.zeros_like(push[:, 0])),
        True,
    )
    backward = backward + product * entering_backward[1][:, None]
    states = forward + backward
    power = taken_together(jnp.sum(states * states, axis=-1, keepdims=True), "width") / (
        states.shape[-1] * lax.axis_size("width")
    )
    mixed_out = (states * lax.rsqrt(power + 1e-06) * norm_gain).astype(jnp.bfloat16)
    return mixed_out


def solution(mesh):
    return jax.shard_map(
        per_device,
        mesh=mesh,
        in_specs=(P(None, "seq", "width"), P(None, "seq", "width"), P("width")),
        out_specs=P(None, "seq", "width"),
        check_vma=False,
    )
```

profile of v0, /device:TPU:1, one launch (start us, length us, event | category | flops | bytes accessed | tf_op | source)
XLA Modules:
  0.0 174.3 jit_solution(18346466432469344434)
XLA Ops:
  0.0 1.4 multiply_exponential_fusion
  2.8 2.1 %slice.904 = f32[1,1023,128]{2,1,0:T(8,128)} slice(f32[1,2048,128]{2,1,0:T(8,128)S(1)} %multiply_exponential_fusion), slice={[0:1:1], [1:2046:2], [0:128:1]} | slice | bytes 1047552 | tf_op jit(solution)/shard_map/slice | solution.py:73
  4.9 5.2 %reverse.13 = f32[1,2048,128]{2,1,0:T(8,128)} reverse(bf16[1,2048,128]{2,1,0:T(8,128)(2,1)S(1)} %copy-done.9), dimensions={1} | reverse | bytes 1572864 | tf_op jit(solution)/shard_map/reverse
  10.1 1.3 broadcast_multiply_fusion
  11.4 2.1 %slice.986 = f32[1,1023,128]{2,1,0:T(8,128)} slice(f32[1,2048,128]{2,1,0:T(8,128)S(1)} %broadcast_multiply_fusion), slice={[0:1:1], [2:2048:2], [0:128:1]} | slice | bytes 1047552 | tf_op jit(solution)/shard_map/slice | solution.py:73
  13.4 2.0 %slice.908 = f32[1,1024,128]{2,1,0:T(8,128)} slice(f32[1,2048,128]{2,1,0:T(8,128)S(1)} %broadcast_multiply_fusion), slice={[0:1:1], [1:2048:2], [0:128:1]} | slice | bytes 1048576 | tf_op jit(solution)/shard_map/slice | solution.py:73
  15.5 2.0 %slice.907 = f32[1,1024,128]{2,1,0:T(8,128)} slice(f32[1,2048,128]{2,1,0:T(8,128)S(1)} %broadcast_multiply_fusion), slice={[0:1:1], [0:2047:2], [0:128:1]} | slice | bytes 1048576 | tf_op jit(solution)/shard_map/slice | solution.py:73
  17.5 2.6 %slice.910 = f32[1,1024,128]{2,1,0:T(8,128)} reverse(f32[1,1024,128]{2,1,0:T(8,128)S(1)} %slice.782), dimensions={1} | reverse | bytes 1048576 | tf_op jit(solution)/shard_map/slice | solution.py:73
  20.1 2.6 %slice.906 = f32[1,1024,128]{2,1,0:T(8,128)} reverse(f32[1,1024,128]{2,1,0:T(8,128)S(1)} %slice.786), dimensions={1} | reverse | bytes 1048576 | tf_op jit(solution)/shard_map/slice | solution.py:73
  22.7 1.6 fusion.18
  24.7 1.4 slice.912
  26.1 1.3 slice.911
  27.4 1.4 slice.984
  29.2 1.4 slice.913
  30.6 1.0 fusion.20
  33.9 2.7 %slice.905 = f32[1,1023,128]{2,1,0:T(8,128)} reverse(f32[1,1023,128]{2,1,0:T(8,128)S(1)} %copy-done.11), dimensions={1} | reverse | bytes 1047552 | tf_op jit(solution)/shard_map/slice | solution.py:73
  41.4 1.0 pad.352
  42.5 2.6 %pad.353 = f32[1,1024,128]{2,1,0:T(8,128)} pad(f32[1,512,128]{2,1,0:T(8,128)} %add.566, f32[]{:T(128)} %constant.5.clone.1), padding=0_0_0x1_0_1x0_0_0 | pad | bytes 786436 | tf_op jit(solution)/shard_map/pad | solution.py:73
  45.1 1.7 pad.331
  46.7 2.0 %add.555 = f32[1,1024,128]{2,1,0:T(8,128)} add(f32[1,1024,128]{2,1,0:T(8,128)S(1)} %pad.330, f32[1,1024,128]{2,1,0:T(8,128)} %pad.331) | non-fusion elementwise | flops 131072 | bytes 1572864 | tf_op jit(solution)/shard_map/add | solution.py:73
  52.1 2.1 %pad.332 = f32[1,2048,128]{2,1,0:T(8,128)S(1)} pad(f32[1,1024,128]{2,1,0:T(8,128)} %pad_maximum_fusion.2, f32[]{:T(128)} %constant.5.clone.1), padding=0_0_0x0_1_1x0_0_0 | pad | bytes 1572868 | tf_op jit(solution)/shard_map/pad | solution.py:73
  54.2 1.9 %pad_maximum_fusion.3 = f32[1,1024,128]{2,1,0:T(8,128)} fusion(f32[1,1023,128]{2,1,0:T(8,128)} %get-tuple-element.13, f32[1,1,128]{2,1,0:T(1,128)S(1)} %get-tuple-element.8), kind=kLoop, calls=%fused_computation.13 | loop fusion | flops 131072 | bytes 1048576 | tf_op jit(solution)/shard_map/concatenate | solution.py:73
  56.1 4.6 %pad.354 = f32[1,2048,128]{2,1,0:T(8,128)} pad(f32[1,1024,128]{2,1,0:T(8,128)} %pad_maximum_fusion.3, f32[]{:T(128)} %constant.5.clone.1), padding=0_0_0x0_1_1x0_0_0 | pad | bytes 1572868 | tf_op jit(solution)/shard_map/pad | solution.py:73
  60.7 4.6 %pad.355 = f32[1,2048,128]{2,1,0:T(8,128)} pad(f32[1,1024,128]{2,1,0:T(8,128)} %add.567, f32[]{:T(128)} %constant.5.clone.1), padding=0_0_0x1_0_1x0_0_0 | pad | bytes 1572868 | tf_op jit(solution)/shard_map/pad | solution.py:73
  65.3 4.6 %pad.333 = f32[1,2048,128]{2,1,0:T(8,128)} pad(f32[1,1024,128]{2,1,0:T(8,128)} %add.555, f32[]{:T(128)} %constant.5.clone.1), padding=0_0_0x1_0_1x0_0_0 | pad | bytes 1572868 | tf_op jit(solution)/shard_map/pad | solution.py:73
  71.8 7.6 %all-to-all-start.1 = ((f32[16,2,128]{2,1,0:T(2,128)}), f32[16,2,128]{2,1,0:T(2,128)S(1)}, u32[]{:S(2)}, u32[]{:S(2)}) async-start(f32[16,2,128]{2,1,0:T(2,128)} %broadcast_in_dim.51), calls=%async_computation.1 | async-start | bytes 32768 | tf_op jit(solution)/shard_map/all_to_all | solution.py:9
  79.4 2.1 %slice.781 = f32[1,1023,128]{2,1,0:T(8,128)} slice(f32[1,2048,128]{2,1,0:T(8,128)S(1)} %multiply_exponential_fusion), slice={[0:1:1], [2:2048:2], [0:128:1]} | slice | bytes 1047552 | tf_op jit(solution)/shard_map/slice | solution.py:64
  81.5 1.1 broadcast_multiply_fusion.1
  82.6 2.1 %slice.862 = f32[1,1023,128]{2,1,0:T(8,128)} slice(f32[1,2048,128]{2,1,0:T(8,128)S(1)} %broadcast_multiply_fusion.1), slice={[0:1:1], [2:2048:2], [0:128:1]} | slice | bytes 1047552 | tf_op jit(solution)/shard_map/slice | solution.py:64
  84.7 2.1 %slice.784 = f32[1,1024,128]{2,1,0:T(8,128)} slice(f32[1,2048,128]{2,1,0:T(8,128)S(1)} %broadcast_multiply_fusion.1), slice={[0:1:1], [1:2048:2], [0:128:1]} | slice | bytes 1048576 | tf_op jit(solution)/shard_map/slice | solution.py:64
  86.8 2.0 %slice.783 = f32[1,1024,128]{2,1,0:T(8,128)} slice(f32[1,2048,128]{2,1,0:T(8,128)S(1)} %broadcast_multiply_fusion.1), slice={[0:1:1], [0:2047:2], [0:128:1]} | slice | bytes 1048576 | tf_op jit(solution)/shard_map/slice | solution.py:64
  88.8 1.3 fusion.17
  91.0 1.4 slice.787
  92.3 1.4 slice.860
  101.5 1.0 add_multiply_fusion.2
  102.5 2.7 %pad.288 = f32[1,2048,128]{2,1,0:T(8,128)} pad(f32[1,1024,128]{2,1,0:T(8,128)S(1)} %pad_maximum_fusion, f32[]{:T(128)} %constant.5.clone.1), padding=0_0_0x0_1_1x0_0_0 | pad | bytes 1572868 | tf_op jit(solution)/shard_map/pad | solution.py:64
  105.3 2.7 %pad.310 = f32[1,2048,128]{2,1,0:T(8,128)} pad(f32[1,1024,128]{2,1,0:T(8,128)S(1)} %pad_maximum_fusion.1, f32[]{:T(128)} %constant.5.clone.1), padding=0_0_0x0_1_1x0_0_0 | pad | bytes 1572868 | tf_op jit(solution)/shard_map/pad | solution.py:64
  108.0 2.7 %pad.311 = f32[1,2048,128]{2,1,0:T(8,128)} pad(f32[1,1024,128]{2,1,0:T(8,128)S(1)} %copy-done.10, f32[]{:T(128)} %constant.5.clone.1), padding=0_0_0x1_0_1x0_0_0 | pad | bytes 1572868 | tf_op jit(solution)/shard_map/pad | solution.py:64
  110.7 4.7 %pad.289 = f32[1,2048,128]{2,1,0:T(8,128)} pad(f32[1,1024,128]{2,1,0:T(8,128)} %add.507, f32[]{:T(128)} %constant.5.clone.1), padding=0_0_0x1_0_1x0_0_0 | pad | bytes 1572868 | tf_op jit(solution)/shard_map/pad | solution.py:64
  116.8 1.1 add.568
  118.4 1.1 add.557
  120.0 5.1 %rev.14 = f32[1,2048,128]{2,1,0:T(8,128)} reverse(f32[1,2048,128]{2,1,0:T(8,128)S(1)} %copy-done.8), dimensions={1} | reverse | bytes 2097152 | tf_op jit(solution)/shard_map/rev | solution.py:73
  125.2 9.0 %rev.13 = f32[1,2048,128]{2,1,0:T(8,128)} reverse(f32[1,2048,128]{2,1,0:T(8,128)} %add.557), dimensions={1} | reverse | bytes 2097152 | tf_op jit(solution)/shard_map/rev | solution.py:73
  134.8 6.6 %all-to-all-start = ((f32[16,2,128]{2,1,0:T(2,128)}), f32[16,2,128]{2,1,0:T(2,128)S(1)}, u32[]{:S(2)}, u32[]{:S(2)}) async-start(f32[16,2,128]{2,1,0:T(2,128)} %broadcast_in_dim.47), calls=%async_computation | async-start | bytes 32768 | tf_op jit(solution)/shard_map/all_to_all | solution.py:9
  141.5 6.3 %all-to-all-done = f32[16,2,128]{2,1,0:T(2,128)S(1)} async-done(((f32[16,2,128]{2,1,0:T(2,128)}), f32[16,2,128]{2,1,0:T(2,128)S(1)}, u32[]{:S(2)}, u32[]{:S(2)}) %all-to-all-start) | async-done | bytes 16416 | tf_op jit(solution)/shard_map/all_to_all | solution.py:9
  148.1 3.2 %multiply_reduce_fusion = (f32[2048]{0:T(1024)S(1)}, f32[1,2048,128]{2,1,0:T(8,128)}) fusion(f32[1,2048,128]{2,1,0:T(8,128)} %rev.13, f32[1,2048,128]{2,1,0:T(8,128)} %rev.14, f32[128]{0:T(128)S(1)} %fusion.14, f32[128]{0:T(128)S(1)} %fusion.15, f32[1,2048,128]{2,1,0:T(8,128)S(1)} %copy-done.6, f32[1,2048,128]{2,1,0:T(8,128)S(1)} %copy-done.7, ...), kind=kLoop, calls=%fused_computation.1 | loop fusion | flops 2357248 | bytes 7349248 | tf_op jit(solution)/shard_map/reduce_sum | solution.py:83
  151.3 19.8 %all_to_all.15 = f32[16,1,2048,1]{2,3,1,0:T(1,128)S(1)} all-to-all(f32[16,1,2048,1]{2,3,1,0:T(1,128)S(1)} %broadcast_in_dim.52), channel_id=1, replica_groups=mesh['seq'=16,'width'=16] {'width'}, dimensions={0} | all-to-all | bytes 262144 | tf_op jit(solution)/shard_map/all_to_all | solution.py:9
  171.9 2.4 %multiply_convert_fusion = bf16[1,2048,128]{2,1,0:T(8,128)(2,1)} fusion(f32[1,2048,128]{2,1,0:T(8,128)} %get-tuple-element.6, f32[128]{0:T(128)S(1)} %copy-done.23, f32[2048]{0:T(1024)S(1)} %add_rsqrt_fusion), kind=kLoop, calls=%fused_computation | loop fusion | flops 786432 | bytes 1581568 | tf_op jit(solution)/shard_map/convert_element_type | solution.py:86
  (392 shorter events, 25.8 us)
Async XLA Ops:
  2.8 2.1 %copy-start.9 = (bf16[1,2048,128]{2,1,0:T(8,128)(2,1)S(1)}, bf16[1,2048,128]{2,1,0:T(8,128)(2,1)}, u32[]{:S(2)}) copy-start(bf16[1,2048,128]{2,1,0:T(8,128)(2,1)} %param.4) | copy-start | bytes 1572868
  29.2 1.4 copy-start.17
  32.9 1.0 copy-start.11
  37.8 1.0 copy-start.21
  37.8 1.1 copy-start.22
  39.7 1.0 copy-start.18
  46.7 2.0 %copy-start = (f32[1,1024,128]{2,1,0:T(8,128)S(1)}, f32[1,1024,128]{2,1,0:T(8,128)}, u32[]{:S(2)}) copy-start(f32[1,1024,128]{2,1,0:T(8,128)} %pad.353) | copy-start | bytes 1572868
  48.7 1.2 copy-start.1
  48.7 1.4 copy-start.14
  48.7 1.5 copy-start.15
  71.8 62.3 %all-to-all-start.1 = ((f32[16,2,128]{2,1,0:T(2,128)}), f32[16,2,128]{2,1,0:T(2,128)S(1)}, u32[]{:S(2)}, u32[]{:S(2)}) async-start(f32[16,2,128]{2,1,0:T(2,128)} %broadcast_in_dim.51), calls=%async_computation.1 | async-start | bytes 32768 | tf_op jit(solution)/shard_map/all_to_all | solution.py:9
  97.8 1.0 copy-start.19
  97.8 1.0 copy-start.20
  100.1 1.2 copy-start.12
  100.1 1.4 copy-start.13
  102.5 2.7 %copy-start.16 = (f32[1,1023,128]{2,1,0:T(8,128)S(1)}, f32[1,1023,128]{2,1,0:T(8,128)}, u32[]{:S(2)}) copy-start(f32[1,1023,128]{2,1,0:T(8,128)} %get-tuple-element.9) | copy-start | bytes 1571332
  105.3 2.7 %copy-start.10 = (f32[1,1024,128]{2,1,0:T(8,128)S(1)}, f32[1,1024,128]{2,1,0:T(8,128)}, u32[]{:S(2)}) copy-start(f32[1,1024,128]{2,1,0:T(8,128)} %add.519) | copy-start | bytes 1572868
  108.0 8.8 %copy-start.4 = (f32[1,2048,128]{2,1,0:T(8,128)S(1)}, f32[1,2048,128]{2,1,0:T(8,128)}, u32[]{:S(2)}) copy-start(f32[1,2048,128]{2,1,0:T(8,128)} %pad.355) | copy-start | bytes 3145732
  110.7 6.1 %copy-start.2 = (f32[1,2048,128]{2,1,0:T(8,128)S(1)}, f32[1,2048,128]{2,1,0:T(8,128)}, u32[]{:S(2)}) copy-start(f32[1,2048,128]{2,1,0:T(8,128)} %pad.354) | copy-start | bytes 3145732
  116.8 1.6 copy-start.3
  118.4 1.6 copy-start.8
  120.0 28.1 %copy-start.7 = (f32[1,2048,128]{2,1,0:T(8,128)S(1)}, f32[1,2048,128]{2,1,0:T(8,128)}, u32[]{:S(2)}) copy-start(f32[1,2048,128]{2,1,0:T(8,128)} %pad.311) | copy-start | bytes 3145732
  125.2 22.9 %copy-start.5 = (f32[1,2048,128]{2,1,0:T(8,128)S(1)}, f32[1,2048,128]{2,1,0:T(8,128)}, u32[]{:S(2)}) copy-start(f32[1,2048,128]{2,1,0:T(8,128)} %pad.288) | copy-start | bytes 3145732
  125.2 22.9 %copy-start.6 = (f32[1,2048,128]{2,1,0:T(8,128)S(1)}, f32[1,2048,128]{2,1,0:T(8,128)}, u32[]{:S(2)}) copy-start(f32[1,2048,128]{2,1,0:T(8,128)} %pad.310) | copy-start | bytes 3145732
  134.8 13.1 %all-to-all-start = ((f32[16,2,128]{2,1,0:T(2,128)}), f32[16,2,128]{2,1,0:T(2,128)S(1)}, u32[]{:S(2)}, u32[]{:S(2)}) async-start(f32[16,2,128]{2,1,0:T(2,128)} %broadcast_in_dim.47), calls=%async_computation | async-start | bytes 32768 | tf_op jit(solution)/shard_map/all_to_all | solution.py:9
  171.3 0.7 copy-start.23
where the time goes:
time: 176 us; the launch traced here: 174 us
  local copies, waits for them, and re-layouts  100 us (57%)
  other arithmetic  31.5 us (18%)
  blocking collectives  19.8 us (11%)
  starting transfers between devices  14.2 us (8%)
  waiting for transfers between devices  6.32 us (4%)
  between operations  2.08 us (1%)
    slice x76, local copies, waits for them, and re-layouts, per_device(): lax.associative_scan(join_pair, (keep, push), axis=1, reverse=True)  23.8 us
    pad x40, local copies, waits for them, and re-layouts, per_device(): lax.associative_scan(join_pair, (keep, push), axis=1, reverse=True)  21.6 us
    all_to_all x1, blocking collectives, copy_for_each(): lax.all_to_all(jnp.broadcast_to(x[None], (length, *x.shape)), axis, 0, 0,...  19.8 us
    slice x76, local copies, waits for them, and re-layouts, per_device(): product, forward = lax.associative_scan(join_pair, (keep, push), axis=1)  15.6 us
    all_to_all x2, starting transfers between devices, copy_for_each(): lax.all_to_all(jnp.broadcast_to(x[None], (length, *x.shape)), axis, 0, 0,...  14.2 us
    rev x2, local copies, waits for them, and re-layouts, per_device(): lax.associative_scan(join_pair, (keep, push), axis=1, reverse=True)  14.1 us
    pad x40, local copies, waits for them, and re-layouts, per_device(): product, forward = lax.associative_scan(join_pair, (keep, push), axis=1)  13.4 us
    mul x44, other arithmetic, join_pair(): return (earlier[0] * later[0], later[0] * earlier[1] + later[1])  7.33 us
  transfers between devices with their start and end apart: 2, of which 1 were waited for; matrix products, arithmetic and copies ran while one was open for 29% of the time, Pallas kernels for 0%

commit v1 on v0

v1 whole, which is shorter than its diff:
```python
import functools

import jax
import jax.numpy as jnp
from jax import lax
from jax.experimental import pallas as pl
from jax.experimental.pallas import tpu as pltpu
from jax.sharding import PartitionSpec as P

LANES = 128
SUB = 8
F32 = jnp.float32
VMEM = pl.BlockSpec(memory_space=pltpu.VMEM)
SMEM = pl.BlockSpec(memory_space=pltpu.SMEM)


def groups_of(rows):
    steps = rows // SUB
    short = steps // 4 - 4
    assert rows % SUB == 0 and short % 8 == 4 and short + 68 <= LANES
    cuts, at = [], 0
    for length in (short, short, short + 8, short + 8):
        cuts.append((at * SUB, at, length))
        at += length
    assert at == steps
    return cuts


def rows_at(group, step):
    first, _, length = group
    return pl.ds(first + step, SUB, stride=length)


def earlier_sublanes(x, by, fill):
    row = lax.broadcasted_iota(jnp.int32, x.shape, 0)
    return jnp.where(row >= by, pltpu.roll(x, by, 0), fill)


def later_sublanes(x, by, fill):
    row = lax.broadcasted_iota(jnp.int32, x.shape, 0)
    return jnp.where(row < SUB - by, pltpu.roll(x, SUB - by, 0), fill)


def scan_sublanes(product, total, shifted):
    for by in (1, 2, 4):
        total = total + product * shifted(total, by, 0.0)
        product = product * shifted(product, by, 1.0)
    return product, total


def all_steps(groups, body, state, reverse=False):
    shortest = min(length for _, _, length in groups)
    tail = range(shortest, max(length for _, _, length in groups))
    state = list(state)

    def tails(order):
        for step in order:
            for g, (_, _, length) in enumerate(groups):
                if step < length:
                    state[g] = body(g, step, state[g])

    if reverse:
        tails(reversed(tail))

    def one(i, carry):
        step = shortest - 1 - i if reverse else i
        return tuple(body(g, step, carry[g]) for g in range(len(groups)))

    state = list(lax.fori_loop(0, shortest, one, tuple(state), unroll=4))
    if not reverse:
        tails(tail)
    return state


def summary_kernel(total_length, leak_ref, signal_ref, ends_ref, parts_ref, keep_ref, push_ref, rows_ref):
    rows = leak_ref.shape[0]
    groups = groups_of(rows)
    scale = total_length ** (-0.5)

    def widen(i, _):
        at = pl.ds(pl.multiple_of(i * 16, 16), 16)
        rows_ref[at, :] = signal_ref[at, :].astype(F32) * scale
        return 0

    lax.fori_loop(0, rows // 16, widen, 0, unroll=8)

    def body(g, step, state):
        product, forward, backward = state
        keep = jnp.exp(-leak_ref[rows_at(groups[g], step), :] / total_length)
        push = rows_ref[rows_at(groups[g], step), :]
        keep_ref[groups[g][1] + step] = keep
        push_ref[groups[g][1] + step] = push
        return (product * keep, forward * keep + push, backward + product * push)

    zero = jnp.zeros((SUB, LANES), F32)
    state = all_steps(groups, body, [(zero + 1.0, zero, zero)] * len(groups))
    ends = []
    for g, (product, forward, backward) in enumerate(state):
        whole, forwards = scan_sublanes(product, forward, earlier_sublanes)
        turned, backwards = scan_sublanes(product, backward, later_sublanes)
        parts_ref[4 * g] = whole
        parts_ref[4 * g + 1] = forwards
        parts_ref[4 * g + 2] = turned
        parts_ref[4 * g + 3] = backwards
        ends.append((whole[SUB - 1 :], forwards[SUB - 1 :], backwards[:1]))
    product, forward, backward = ends[0][0], ends[0][1], ends[-1][2]
    for whole, forwards, _ in ends[1:]:
        product, forward = product * whole, forward * whole + forwards
    for whole, _, backwards in reversed(ends[:-1]):
        backward = backwards + whole * backward
    ends_ref[...] = jnp.concatenate([product, forward, backward, jnp.zeros_like(product)], axis=0)


def states_kernel(here_ref, all_ends_ref, parts_ref, keep_ref, push_ref, states_ref, squares_ref):
    groups = groups_of(keep_ref.shape[0] * SUB)
    here = here_ref[0]
    devices = all_ends_ref.shape[0]
    forward = jnp.zeros((1, LANES), F32)
    backward = jnp.zeros((1, LANES), F32)
    for d in range(devices):
        joined = forward * all_ends_ref[d, 0:1] + all_ends_ref[d, 1:2]
        forward = jnp.where(d < here, joined, forward)
        e = devices - 1 - d
        joined = backward * all_ends_ref[e, 0:1] + all_ends_ref[e, 2:3]
        backward = jnp.where(e > here, joined, backward)

    entering_forward, entering_backward = [], [None] * len(groups)
    for g in range(len(groups)):
        whole, forwards = parts_ref[4 * g], parts_ref[4 * g + 1]
        entering_forward.append(
            earlier_sublanes(forwards, 1, 0.0) + earlier_sublanes(whole, 1, 1.0) * forward
        )
        forward = forwards[SUB - 1 :] + whole[SUB - 1 :] * forward
    for g in reversed(range(len(groups))):
        whole, backwards = parts_ref[4 * g + 2], parts_ref[4 * g + 3]
        entering_backward[g] = (
            later_sublanes(backwards, 1, 0.0) + later_sublanes(whole, 1, 1.0) * backward
        )
        backward = backwards[:1] + whole[:1] * backward

    def forth(g, step, state):
        at = groups[g][1] + step
        state = state * keep_ref[at] + push_ref[at]
        states_ref[at] = state
        return state

    all_steps(groups, forth, entering_forward)
    lane = lax.broadcasted_iota(jnp.int32, (SUB, LANES), 1)
    short = groups[0][2]

    def back(g, step, state):
        state, sums = state
        at = groups[g][1] + step
        state = state * keep_ref[at] + push_ref[at]
        both = states_ref[at] + state
        states_ref[at] = both
        power = jnp.sum(both * both, axis=1, keepdims=True)
        sums = jnp.where(lane == step + (short if g >= 2 else 0), power, sums)
        return state, sums

    zero = jnp.zeros((SUB, LANES), F32)
    done = all_steps(groups, back, [(b, zero) for b in entering_backward], reverse=True)
    for half in (0, 1):
        squares_ref[pl.ds(half * SUB, SUB), :] = jnp.where(lane < short, done[half][1], done[half + 2][1])


def norm_kernel(channels, all_squares_ref, states_ref, gain_ref, out_ref, rows_ref):
    rows = out_ref.shape[0]
    groups = groups_of(rows)
    short = groups[0][2]
    power = jnp.sum(all_squares_ref[...], axis=0) / channels
    scale = lax.rsqrt(power + 1e-06)
    halves = (scale[:SUB], scale[SUB:])
    gain = jnp.broadcast_to(gain_ref[...], (SUB, LANES))
    for g, (_, first, length) in enumerate(groups):
        for step in range(length):
            lane = step + (short if g >= 2 else 0)
            factor = jnp.broadcast_to(halves[g % 2][:, lane : lane + 1], (SUB, LANES))
            rows_ref[rows_at(groups[g], step), :] = states_ref[first + step] * factor * gain

    def narrow(i, _):
        at = pl.ds(pl.multiple_of(i * 16, 16), 16)
        out_ref[at, :] = rows_ref[at, :].astype(out_ref.dtype)
        return 0

    lax.fori_loop(0, rows // 16, narrow, 0, unroll=8)


def params():
    return pltpu.CompilerParams(vmem_limit_bytes=12 * 1024 * 1024)


def copies(x, axis):
    x = jnp.broadcast_to(x[None], (lax.axis_size(axis), *x.shape))
    return lax.all_to_all(x, axis, 0, 0, tiled=True)


def per_device(leak_rate, signal_in, norm_gain):
    rows, channels = leak_rate.shape[1], leak_rate.shape[2]
    total_length = rows * lax.axis_size("seq")
    steps = rows // SUB
    blocks = jax.ShapeDtypeStruct((steps, SUB, LANES), F32)
    ends, parts, keep, push = pl.pallas_call(
        functools.partial(summary_kernel, total_length),
        out_shape=(
            jax.ShapeDtypeStruct((4, LANES), F32),
            jax.ShapeDtypeStruct((16, SUB, LANES), F32),
            blocks,
            blocks,
        ),
        in_specs=[VMEM] * 2,
        out_specs=(VMEM,) * 4,
        scratch_shapes=[pltpu.VMEM((rows, LANES), F32)],
        compiler_params=params(),
        name="summary",
    )(leak_rate[0], signal_in[0])
    all_ends = copies(ends, "seq")
    here = lax.axis_index("seq").astype(jnp.int32).reshape(1)
    states, squares = pl.pallas_call(
        states_kernel,
        out_shape=(blocks, jax.ShapeDtypeStruct((2 * SUB, LANES), F32)),
        in_specs=[SMEM] + [VMEM] * 4,
        out_specs=(VMEM,) * 2,
        compiler_params=params(),
        name="states",
    )(here, all_ends, parts, keep, push)
    all_squares = copies(squares, "width")
    mixed = pl.pallas_call(
        functools.partial(norm_kernel, channels * lax.axis_size("width")),
        out_shape=jax.ShapeDtypeStruct((rows, LANES), jnp.bfloat16),
        in_specs=[VMEM] * 3,
        out_specs=VMEM,
        scratch_shapes=[pltpu.VMEM((rows, LANES), F32)],
        compiler_params=params(),
        name="norm",
    )(all_squares, states, norm_gain.reshape(1, channels))
    return mixed[None]


def solution(mesh):
    return jax.shard_map(
        per_device,
        mesh=mesh,
        in_specs=(P(None, "seq", "width"), P(None, "seq", "width"), P("width")),
        out_specs=P(None, "seq", "width"),
        check_vma=False,
    )
```

time: 176 us -> 42.1 us (0.24)
  local copies, waits for them, and re-layouts: 100 us -> 3.56 us
  other arithmetic: 31.5 us -> 0 us
  starting transfers between devices: 14.2 us -> 7.57 us
  Pallas kernels: 0 us -> 5.01 us
  between operations: 2.08 us -> 0.02 us
    slice x154 -> x0, local copies, waits for them, and re-layouts: 39.4 us -> none  [the longest x76 23.8 us: per_device(): lax.associative_scan(join_pair, (keep, push), axis=1, reverse=True)]
    pad x80 -> x0, local copies, waits for them, and re-layouts: 35 us -> none  [the longest x40 21.6 us: per_device(): lax.associative_scan(join_pair, (keep, push), axis=1, reverse=True)]
    rev x2 -> x0, local copies, waits for them, and re-layouts: 14.1 us -> none  [per_device(): lax.associative_scan(join_pair, (keep, push), axis=1, reverse=True)]
    mul x47 -> x0, other arithmetic: 8.46 us -> none  [the longest x44 7.33 us: join_pair(): return (earlier[0] * later[0], later[0] * earlier[1] + later[1])]
    add x40 -> x0, other arithmetic: 7.81 us -> none  [the longest x21 5.9 us: per_device(): lax.associative_scan(join_pair, (keep, push), axis=1, reverse=True)]
    all_to_all x2 -> x1, starting transfers between devices: 14.2 us -> 7.57 us  [copies(): return lax.all_to_all(x, axis, 0, 0, tiled=True)]
    another operation x1 -> x0, local copies, waits for them, and re-layouts: 5.17 us -> none
    pallas_call x0 -> x3, Pallas kernels: none -> 5.01 us  [the longest x1 2.74 us: per_device(): pl.pallas_call(states_kernel, out_shape=(blocks, jax.ShapeDtypeStruct((2...]
  transfers between devices with their start and end apart: 2 -> 1, of which waited for: 1 -> 1; matrix products, arithmetic and copies ran while one was open for 29% -> 0% of each run, Pallas kernels for 0% -> 0%
where the time goes in v1:
time: 42.1 us; the launch traced here: 41.9 us
  blocking collectives  19.2 us (46%)
  starting transfers between devices  7.57 us (18%)
  waiting for transfers between devices  6.47 us (15%)
  Pallas kernels  5.01 us (12%)
  local copies, waits for them, and re-layouts  3.56 us (8%)
    all_to_all x1, blocking collectives, copies(): return lax.all_to_all(x, axis, 0, 0, tiled=True)  19.2 us
    all_to_all x1, starting transfers between devices, copies(): return lax.all_to_all(x, axis, 0, 0, tiled=True)  7.57 us
    all_to_all x1, waiting for transfers between devices, copies(): return lax.all_to_all(x, axis, 0, 0, tiled=True)  6.47 us
    unnamed x6, local copies, waits for them, and re-layouts  2.92 us
    pallas_call x1, Pallas kernels, per_device(): pl.pallas_call(states_kernel, out_shape=(blocks, jax.ShapeDtypeStruct((2...  2.74 us
    pallas_call x1, Pallas kernels, per_device(): pl.pallas_call(functools.partial(norm_kernel, channels * lax.axis_size('w...  1.54 us
  transfers between devices with their start and end apart: 1, of which 1 were waited for; matrix products, arithmetic and copies ran while one was open for 0% of the time, Pallas kernels for 0%

profile of v1, /device:TPU:1, one launch (start us, length us, event | category | flops | bytes accessed | tf_op | source)
XLA Modules:
  0.0 41.9 jit_solution(9766237470297839644)
XLA Ops:
  0.0 0.0 copy-start
  0.0 1.2 %copy-done = f32[1,2048,128]{2,1,0:T(8,128)S(1)} copy-done((f32[1,2048,128]{2,1,0:T(8,128)S(1)}, f32[1,2048,128]{2,1,0:T(8,128)}, u32[]{:S(2)}) %copy-start) | copy-done | bytes 1048600
  1.2 0.0 copy-start.1
  1.2 1.0 %copy-done.1 = bf16[1,2048,128]{2,1,0:T(8,128)(2,1)S(1)} copy-done((bf16[1,2048,128]{2,1,0:T(8,128)(2,1)S(1)}, bf16[1,2048,128]{2,1,0:T(8,128)(2,1)}, u32[]{:S(2)}) %copy-start.1) | copy-done | bytes 524312
  2.3 0.7 %summary.1 = (f32[4,128]{1,0:T(4,128)S(1)}, f32[16,8,128]{2,1,0:T(8,128)S(1)}, f32[256,8,128]{2,1,0:T(8,128)S(1)}, f32[256,8,128]{2,1,0:T(8,128)S(1)}) custom-call(f32[2048,128]{1,0:T(8,128)S(1)} %bitcast.5, bf16[2048,128]{1,0:T(8,128)(2,1)S(1)} %bitcast.6), custom_call_target="tpu_custom_call" | custom-call | tf_op jit(solution)/shard_map/summary/pallas_call | solution.py:203
  3.0 0.6 %broadcast_in_dim.6 = f32[16,4,128]{2,1,0:T(4,128)} broadcast(f32[4,128]{1,0:T(4,128)S(1)} %get-tuple-element.11), dimensions={1,2} | broadcast | bytes 34816 | tf_op jit(solution)/shard_map/broadcast_in_dim | solution.py:194
  3.6 7.6 %all-to-all-start = ((f32[16,4,128]{2,1,0:T(4,128)}), f32[16,4,128]{2,1,0:T(4,128)S(1)}, u32[]{:S(2)}, u32[]{:S(2)}) async-start(f32[16,4,128]{2,1,0:T(4,128)} %broadcast_in_dim.6), calls=%async_computation | async-start | bytes 65536 | tf_op jit(solution)/shard_map/all_to_all | solution.py:195
  11.2 6.5 %all-to-all-done.all_ends_ref = f32[16,4,128]{2,1,0:T(4,128)S(1)} async-done(((f32[16,4,128]{2,1,0:T(4,128)}), f32[16,4,128]{2,1,0:T(4,128)S(1)}, u32[]{:S(2)}, u32[]{:S(2)}) %all-to-all-start) | async-done | bytes 32800 | tf_op jit(solution)/shard_map/all_to_all | solution.py:195
  17.7 2.7 %states.1 = (f32[256,8,128]{2,1,0:T(8,128)S(1)}, f32[16,128]{1,0:T(8,128)S(1)}) custom-call(s32[1]{0:T(128)} %bitcast.here_ref, f32[16,4,128]{2,1,0:T(4,128)S(1)} %all-to-all-done.all_ends_ref, f32[16,8,128]{2,1,0:T(8,128)S(1)} %get-tuple-element.12.parts_ref, f32[256,8,128]{2,1,0:T(8,128)S(1)} %get-tuple-element.13.keep_ref, ...), custom_call_target="tpu_custom_call" | custom-call | tf_op jit(solution)/shard_map/states/pallas_call | solution.py:219
  20.4 19.2 %all_to_all.10.all_squares_ref = f32[16,16,128]{2,1,0:T(8,128)S(1)} all-to-all(f32[16,16,128]{2,1,0:T(8,128)S(1)} %broadcast_in_dim.7), channel_id=1, replica_groups=mesh['seq'=16,'width'=16] {'width'}, dimensions={0} | all-to-all | bytes 262144 | tf_op jit(solution)/shard_map/all_to_all | solution.py:195
  39.7 0.0 copy-start.2
  39.7 0.7 %copy-done.2 = f32[128]{0:T(128)S(1)} copy-done((f32[128]{0:T(128)S(1)}, f32[128]{0:T(128)}, u32[]{:S(2)}) %copy-start.2) | copy-done | bytes 536
  40.3 1.5 %norm.1 = bf16[2048,128]{1,0:T(8,128)(2,1)} custom-call(f32[16,16,128]{2,1,0:T(8,128)S(1)} %all_to_all.10.all_squares_ref, f32[256,8,128]{2,1,0:T(8,128)S(1)} %get-tuple-element.16.states_ref, f32[1,128]{1,0:T(1,128)S(1)} %bitcast.7), custom_call_target="tpu_custom_call" | custom-call | tf_op jit(solution)/shard_map/norm/pallas_call | solution.py:228
  (1 shorter events, 0.0 us)
Async XLA Ops:
  0.0 1.2 %copy-start = (f32[1,2048,128]{2,1,0:T(8,128)S(1)}, f32[1,2048,128]{2,1,0:T(8,128)}, u32[]{:S(2)}) copy-start(f32[1,2048,128]{2,1,0:T(8,128)} %param.3) | copy-start | bytes 3145732
  1.2 1.0 %copy-start.1 = (bf16[1,2048,128]{2,1,0:T(8,128)(2,1)S(1)}, bf16[1,2048,128]{2,1,0:T(8,128)(2,1)}, u32[]{:S(2)}) copy-start(bf16[1,2048,128]{2,1,0:T(8,128)(2,1)} %param.4) | copy-start | bytes 1572868
  3.6 14.1 %all-to-all-start = ((f32[16,4,128]{2,1,0:T(4,128)}), f32[16,4,128]{2,1,0:T(4,128)S(1)}, u32[]{:S(2)}, u32[]{:S(2)}) async-start(f32[16,4,128]{2,1,0:T(4,128)} %broadcast_in_dim.6), calls=%async_computation | async-start | bytes 65536 | tf_op jit(solution)/shard_map/all_to_all | solution.py:195
  39.7 0.7 %copy-start.2 = (f32[128]{0:T(128)S(1)}, f32[128]{0:T(128)}, u32[]{:S(2)}) copy-start(f32[128]{0:T(128)} %param.5) | copy-start | bytes 1540

commit v2 on v1

v2 whole, which is shorter than its diff:
```python
import functools

import jax
import jax.numpy as jnp
from jax import lax
from jax.experimental import pallas as pl
from jax.experimental.pallas import tpu as pltpu
from jax.sharding import PartitionSpec as P

LANES = 128
SUB = 8
F32 = jnp.float32
VMEM = pl.BlockSpec(memory_space=pltpu.VMEM)
SMEM = pl.BlockSpec(memory_space=pltpu.SMEM)
HBM = pl.BlockSpec(memory_space=pltpu.HBM)


def groups_of(rows):
    steps = rows // SUB
    short = steps // 4 - 4
    assert rows % SUB == 0 and short % 8 == 4 and short + 68 <= LANES
    cuts, at = [], 0
    for length in (short, short, short + 8, short + 8):
        cuts.append((at * SUB, at, length))
        at += length
    assert at == steps
    return cuts


def rows_at(group, step):
    first, _, length = group
    return pl.ds(first + step, SUB, stride=length)


def earlier_sublanes(x, by, fill):
    row = lax.broadcasted_iota(jnp.int32, x.shape, 0)
    return jnp.where(row >= by, pltpu.roll(x, by, 0), fill)


def later_sublanes(x, by, fill):
    row = lax.broadcasted_iota(jnp.int32, x.shape, 0)
    return jnp.where(row < SUB - by, pltpu.roll(x, SUB - by, 0), fill)


def scan_sublanes(product, total, shifted):
    for by in (1, 2, 4):
        total = total + product * shifted(total, by, 0.0)
        product = product * shifted(product, by, 1.0)
    return product, total


def all_steps(groups, body, state, reverse=False):
    state = dict(state)
    longest = max(groups[g][2] for g in state)
    for step in reversed(range(longest)) if reverse else range(longest):
        for g in state:
            if step < groups[g][2]:
                state[g] = body(g, step, state[g])
    return state


def rows_of(group):
    first, _, length = group
    return pl.ds(first, length * SUB)


def summary_kernel(
    total_length,
    here_ref,
    leak_hbm,
    signal_hbm,
    gain_hbm,
    ends_ref,
    parts_ref,
    keep_ref,
    push_ref,
    gain_ref,
    leak_ref,
    signal_ref,
    rows_ref,
    arrived,
    gain_arrived,
):
    groups = groups_of(leak_ref.shape[0])
    scale = total_length ** (-0.5)
    loads = []
    for g, group in enumerate(groups):
        at = rows_of(group)
        loads.append(
            (
                pltpu.make_async_copy(leak_hbm.at[at], leak_ref.at[at], arrived.at[0, g]),
                pltpu.make_async_copy(signal_hbm.at[at], signal_ref.at[at], arrived.at[1, g]),
            )
        )
        for load in loads[-1]:
            load.start()
    gain_load = pltpu.make_async_copy(gain_hbm, gain_ref, gain_arrived)
    gain_load.start()

    def body(g, step, state):
        product, forward, backward = state
        keep = jnp.exp(-leak_ref[rows_at(groups[g], step), :] / total_length)
        push = rows_ref[rows_at(groups[g], step), :]
        keep_ref[groups[g][1] + step] = keep
        push_ref[groups[g][1] + step] = push
        return (product * keep, forward * keep + push, backward + product * push)

    zero = jnp.zeros((SUB, LANES), F32)
    state = {}
    for pair in ((0, 1), (2, 3)):
        for g in pair:
            for load in loads[g]:
                load.wait()
        for g in pair:
            first, _, length = groups[g]
            for row in range(first, first + length * SUB, 16):
                at = pl.ds(row, 16)
                rows_ref[at, :] = signal_ref[at, :].astype(F32) * scale
        state |= all_steps(groups, body, {g: (zero + 1.0, zero, zero) for g in pair})
    ends = []
    for g in range(len(groups)):
        product, forward, backward = state[g]
        whole, forwards = scan_sublanes(product, forward, earlier_sublanes)
        turned, backwards = scan_sublanes(product, backward, later_sublanes)
        parts_ref[4 * g] = whole
        parts_ref[4 * g + 1] = forwards
        parts_ref[4 * g + 2] = turned
        parts_ref[4 * g + 3] = backwards
        ends.append((whole[SUB - 1 :], forwards[SUB - 1 :], backwards[:1]))
    product, forward, backward = ends[0][0], ends[0][1], ends[-1][2]
    for whole, forwards, _ in ends[1:]:
        product, forward = product * whole, forward * whole + forwards
    for whole, _, backwards in reversed(ends[:-1]):
        backward = backwards + whole * backward
    row = lax.broadcasted_iota(jnp.int32, (SUB, LANES), 0)
    packed = jnp.where(row == 0, product, jnp.where(row == 1, forward, backward))
    for copy in range(ends_ref.shape[0]):
        ends_ref[copy] = packed
    parts_ref[4 * len(groups)] = zero + here_ref[0].astype(F32)
    gain_load.wait()


def states_kernel(all_ends_ref, parts_ref, keep_ref, push_ref, states_ref, squares_ref):
    groups = groups_of(keep_ref.shape[0] * SUB)
    here = parts_ref[4 * len(groups), 0:1]
    devices = all_ends_ref.shape[0]
    forward = jnp.zeros((1, LANES), F32)
    backward = jnp.zeros((1, LANES), F32)
    for d in range(devices):
        joined = forward * all_ends_ref[d, 0:1] + all_ends_ref[d, 1:2]
        forward = jnp.where(d < here, joined, forward)
        e = devices - 1 - d
        joined = backward * all_ends_ref[e, 0:1] + all_ends_ref[e, 2:3]
        backward = jnp.where(e > here, joined, backward)

    entering_forward, entering_backward = [], [None] * len(groups)
    for g in range(len(groups)):
        whole, forwards = parts_ref[4 * g], parts_ref[4 * g + 1]
        entering_forward.append(
            earlier_sublanes(forwards, 1, 0.0) + earlier_sublanes(whole, 1, 1.0) * forward
        )
        forward = forwards[SUB - 1 :] + whole[SUB - 1 :] * forward
    for g in reversed(range(len(groups))):
        whole, backwards = parts_ref[4 * g + 2], parts_ref[4 * g + 3]
        entering_backward[g] = (
            later_sublanes(backwards, 1, 0.0) + later_sublanes(whole, 1, 1.0) * backward
        )
        backward = backwards[:1] + whole[:1] * backward

    def forth(g, step, state):
        at = groups[g][1] + step
        state = state * keep_ref[at] + push_ref[at]
        states_ref[at] = state
        return state

    all_steps(groups, forth, dict(enumerate(entering_forward)))
    lane = lax.broadcasted_iota(jnp.int32, (SUB, LANES), 1)
    short = groups[0][2]

    def back(g, step, state):
        state, sums = state
        at = groups[g][1] + step
        state = state * keep_ref[at] + push_ref[at]
        both = states_ref[at] + state
        states_ref[at] = both
        power = jnp.sum(both * both, axis=1, keepdims=True)
        sums = jnp.where(lane == step + (short if g >= 2 else 0), power, sums)
        return state, sums

    zero = jnp.zeros((SUB, LANES), F32)
    done = all_steps(groups, back, {g: (b, zero) for g, b in enumerate(entering_backward)}, reverse=True)
    for half in (0, 1):
        squares = jnp.where(lane < short, done[half][1], done[half + 2][1])
        for copy in range(squares_ref.shape[0]):
            squares_ref[copy, pl.ds(half * SUB, SUB), :] = squares


def norm_kernel(channels, all_squares_ref, states_ref, gain_ref, out_hbm, rows_ref, out_ref, sent):
    groups = groups_of(rows_ref.shape[0])
    short = groups[0][2]
    power = jnp.sum(all_squares_ref[...], axis=0) / channels
    scale = lax.rsqrt(power + 1e-06)
    halves = (scale[:SUB], scale[SUB:])
    gain = jnp.broadcast_to(gain_ref[...], (SUB, LANES))
    stores = []
    for g, (first, at, length) in enumerate(groups):
        for step in range(length):
            lane = step + (short if g >= 2 else 0)
            factor = jnp.broadcast_to(halves[g % 2][:, lane : lane + 1], (SUB, LANES))
            rows_ref[rows_at(groups[g], step), :] = states_ref[at + step] * factor * gain
        for row in range(first, first + length * SUB, 16):
            here = pl.ds(row, 16)
            out_ref[here, :] = rows_ref[here, :].astype(out_ref.dtype)
        rows = rows_of(groups[g])
        stores.append(pltpu.make_async_copy(out_ref.at[rows], out_hbm.at[rows], sent.at[g]))
        stores[-1].start()
    for store in stores:
        store.wait()


def params():
    return pltpu.CompilerParams(vmem_limit_bytes=12 * 1024 * 1024)


def exchanged(x, axis):
    return lax.all_to_all(x, axis, 0, 0, tiled=True)


def per_device(leak_rate, signal_in, norm_gain):
    rows, channels = leak_rate.shape[1], leak_rate.shape[2]
    total_length = rows * lax.axis_size("seq")
    blocks = jax.ShapeDtypeStruct((rows // SUB, SUB, LANES), F32)
    here = lax.axis_index("seq").astype(jnp.int32).reshape(1)
    operands = (leak_rate[0], signal_in[0], norm_gain.reshape(1, channels))
    ends, parts, keep, push, gain = pl.pallas_call(
        functools.partial(summary_kernel, total_length),
        out_shape=(
            jax.ShapeDtypeStruct((lax.axis_size("seq"), SUB, LANES), F32),
            jax.ShapeDtypeStruct((17, SUB, LANES), F32),
            blocks,
            blocks,
            jax.ShapeDtypeStruct((1, LANES), F32),
        ),
        in_specs=[SMEM] + [HBM] * 3,
        out_specs=(VMEM,) * 5,
        scratch_shapes=[
            pltpu.VMEM((rows, LANES), F32),
            pltpu.VMEM((rows, LANES), signal_in.dtype),
            pltpu.VMEM((rows, LANES), F32),
            pltpu.SemaphoreType.DMA((2, 4)),
            pltpu.SemaphoreType.DMA,
        ],
        compiler_params=params(),
        name="summary",
    )(here, *(pltpu.with_memory_space_constraint(x, pltpu.HBM) for x in operands))
    all_ends = exchanged(ends, "seq")
    states, squares = pl.pallas_call(
        states_kernel,
        out_shape=(blocks, jax.ShapeDtypeStruct((lax.axis_size("width"), 2 * SUB, LANES), F32)),
        in_specs=[VMEM] * 4,
        out_specs=(VMEM,) * 2,
        compiler_params=params(),
        name="states",
    )(all_ends, parts, keep, push)
    all_squares = exchanged(squares, "width")
    mixed = pl.pallas_call(
        functools.partial(norm_kernel, channels * lax.axis_size("width")),
        out_shape=jax.ShapeDtypeStruct((rows, LANES), jnp.bfloat16),
        in_specs=[VMEM] * 3,
        out_specs=HBM,
        scratch_shapes=[
            pltpu.VMEM((rows, LANES), F32),
            pltpu.VMEM((rows, LANES), jnp.bfloat16),
            pltpu.SemaphoreType.DMA((4,)),
        ],
        compiler_params=params(),
        name="norm",
    )(all_squares, states, gain)
    return mixed[None]


def solution(mesh):
    return jax.shard_map(
        per_device,
        mesh=mesh,
        in_specs=(P(None, "seq", "width"), P(None, "seq", "width"), P("width")),
        out_specs=P(None, "seq", "width"),
        check_vma=False,
    )
```

time: 42.1 us -> 37.1 us (0.88)
  blocking collectives: 19.2 us -> 33.2 us
  starting transfers between devices: 7.57 us -> 0 us
  waiting for transfers between devices: 6.47 us -> 0 us
  local copies, waits for them, and re-layouts: 3.56 us -> 0 us
  Pallas kernels: 5.01 us -> 3.73 us
    all_to_all x1 -> x2, blocking collectives: 19.2 us -> 33.2 us  [exchanged(): return lax.all_to_all(x, axis, 0, 0, tiled=True)]
    all_to_all x1 -> x0, starting transfers between devices: 7.57 us -> none  [copies(): return lax.all_to_all(x, axis, 0, 0, tiled=True)]
    all_to_all x1 -> x0, waiting for transfers between devices: 6.47 us -> none  [copies(): return lax.all_to_all(x, axis, 0, 0, tiled=True)]
    unnamed x6 -> x0, local copies, waits for them, and re-layouts: 2.92 us -> none
    pallas_call x1, Pallas kernels: 2.74 us -> 0.6 us  [per_device(): pl.pallas_call(states_kernel, out_shape=(blocks, jax.ShapeDtypeStruct((la...]
    pallas_call x1, Pallas kernels: 0.73 us -> 1.79 us  [per_device(): pl.pallas_call(functools.partial(summary_kernel, total_length), out_shape...]
    broadcast_in_dim x2 -> x0, local copies, waits for them, and re-layouts: 0.64 us -> none  [copies(): x = jnp.broadcast_to(x[None], (lax.axis_size(axis), *x.shape))]
  transfers between devices with their start and end apart: 1 -> 0, of which waited for: 1 -> 0; matrix products, arithmetic and copies ran while one was open for 0% -> 0% of each run, Pallas kernels for 0% -> 0%
where the time goes in v2:
time: 37.1 us; the launch traced here: 36.9 us
  blocking collectives  33.2 us (89%)
  Pallas kernels  3.73 us (10%)
    all_to_all x2, blocking collectives, exchanged(): return lax.all_to_all(x, axis, 0, 0, tiled=True)  33.2 us
    pallas_call x1, Pallas kernels, per_device(): pl.pallas_call(functools.partial(summary_kernel, total_length), out_shape...  1.79 us
    pallas_call x1, Pallas kernels, per_device(): pl.pallas_call(functools.partial(norm_kernel, channels * lax.axis_size('w...  1.34 us

profile of v2, /device:TPU:1, one launch (start us, length us, event | category | flops | bytes accessed | tf_op | source)
XLA Modules:
  0.0 36.9 jit_solution(6656343989150774262)
XLA Ops:
  0.0 1.8 %summary.1 = (f32[16,8,128]{2,1,0:T(8,128)S(1)}, f32[17,8,128]{2,1,0:T(8,128)S(1)}, f32[256,8,128]{2,1,0:T(8,128)S(1)}, f32[256,8,128]{2,1,0:T(8,128)S(1)}, f32[1,128]{1,0:T(1,128)S(1)}) custom-call(s32[1]{0:T(128)} %bitcast.here_ref, f32[2048,128]{1,0:T(8,128)} %bitcast.5, bf16[2048,128]{1,0:T(8,128)(2,1)} %bitcast.6, f32[1,128]{1,0:T(1,128)} %bitcast.7), custom_call_target="tpu_custom_call" | custom-call | tf_op jit(solution)/shard_map/summary/pallas_call | solution.py:235
  1.8 13.9 %all_to_all.10.all_ends_ref = f32[16,8,128]{2,1,0:T(8,128)S(1)} all-to-all(f32[16,8,128]{2,1,0:T(8,128)S(1)} %get-tuple-element.12), channel_id=1, replica_groups=mesh['seq'=16,'width'=16] {'seq'}, dimensions={0} | all-to-all | bytes 131072 | tf_op jit(solution)/shard_map/all_to_all | solution.py:226
  15.7 0.6 %states.1 = (f32[256,8,128]{2,1,0:T(8,128)S(1)}, f32[16,16,128]{2,1,0:T(8,128)S(1)}) custom-call(f32[16,8,128]{2,1,0:T(8,128)S(1)} %all_to_all.10.all_ends_ref, f32[17,8,128]{2,1,0:T(8,128)S(1)} %get-tuple-element.13.parts_ref, f32[256,8,128]{2,1,0:T(8,128)S(1)} %get-tuple-element.14.keep_ref, f32[256,8,128]{2,1,0:T(8,128)S(1)} %get-tuple-element.15.push_ref), custom_call_target="tpu_custom_call" | custom-call | tf_op jit(solution)/shard_map/states/pallas_call | solution.py:257
  16.3 19.3 %all_to_all.11.all_squares_ref = f32[16,16,128]{2,1,0:T(8,128)S(1)} all-to-all(f32[16,16,128]{2,1,0:T(8,128)S(1)} %get-tuple-element.16), channel_id=1, replica_groups=mesh['seq'=16,'width'=16] {'width'}, dimensions={0} | all-to-all | bytes 262144 | tf_op jit(solution)/shard_map/all_to_all | solution.py:226
  35.6 1.3 %norm.1 = bf16[2048,128]{1,0:T(8,128)(2,1)} custom-call(f32[16,16,128]{2,1,0:T(8,128)S(1)} %all_to_all.11.all_squares_ref, f32[256,8,128]{2,1,0:T(8,128)S(1)} %get-tuple-element.17.states_ref, f32[1,128]{1,0:T(1,128)S(1)} %get-tuple-element.18.gain_ref), custom_call_target="tpu_custom_call" | custom-call | tf_op jit(solution)/shard_map/norm/pallas_call | solution.py:266

commit v3 on v2

--- a/solution.py
+++ b/solution.py
@@ -13,6 +13,15 @@
 VMEM = pl.BlockSpec(memory_space=pltpu.VMEM)
 SMEM = pl.BlockSpec(memory_space=pltpu.SMEM)
 HBM = pl.BlockSpec(memory_space=pltpu.HBM)
+
+
+FIRST = {"seq": 10, "width": 9}
+
+
+def order_of(axis):
+    size = lax.axis_size(axis)
+    first = FIRST[axis] % size
+    return [first] + [member for member in range(size) if member != first]
 
 
 def groups_of(rows):
@@ -140,17 +149,18 @@
     gain_load.wait()
 
 
-def states_kernel(all_ends_ref, parts_ref, keep_ref, push_ref, states_ref, squares_ref):
+def states_kernel(order, all_ends_ref, parts_ref, keep_ref, push_ref, states_ref, squares_ref):
     groups = groups_of(keep_ref.shape[0] * SUB)
     here = parts_ref[4 * len(groups), 0:1]
-    devices = all_ends_ref.shape[0]
+    devices = len(order)
+    place = [order.index(d) for d in range(devices)]
     forward = jnp.zeros((1, LANES), F32)
     backward = jnp.zeros((1, LANES), F32)
     for d in range(devices):
-        joined = forward * all_ends_ref[d, 0:1] + all_ends_ref[d, 1:2]
+        joined = forward * all_ends_ref[place[d], 0:1] + all_ends_ref[place[d], 1:2]
         forward = jnp.where(d < here, joined, forward)
         e = devices - 1 - d
-        joined = backward * all_ends_ref[e, 0:1] + all_ends_ref[e, 2:3]
+        joined = backward * all_ends_ref[place[e], 0:1] + all_ends_ref[place[e], 2:3]
         backward = jnp.where(e > here, joined, backward)
 
     entering_forward, entering_backward = [], [None] * len(groups)
@@ -223,7 +233,7 @@
 
 
 def exchanged(x, axis):
-    return lax.all_to_all(x, axis, 0, 0, tiled=True)
+    return lax.all_to_all(x, axis, 0, 0, tiled=True, axis_index_groups=[order_of(axis)])
 
 
 def per_device(leak_rate, signal_in, norm_gain):
@@ -255,7 +265,7 @@
     )(here, *(pltpu.with_memory_space_constraint(x, pltpu.HBM) for x in operands))
     all_ends = exchanged(ends, "seq")
     states, squares = pl.pallas_call(
-        states_kernel,
+        functools.partial(states_kernel, order_of("seq")),
         out_shape=(blocks, jax.ShapeDtypeStruct((lax.axis_size("width"), 2 * SUB, LANES), F32)),
         in_specs=[VMEM] * 4,
         out_specs=(VMEM,) * 2,

time: 37.1 us -> 30.4 us (0.82)
  blocking collectives: 33.2 us -> 26.5 us
    all_to_all x2, blocking collectives: 33.2 us -> 26.5 us  [exchanged(): lax.all_to_all(x, axis, 0, 0, tiled=True, axis_index_groups=[order_of(axi...]
where the time goes in v3:
time: 30.4 us; the launch traced here: 30.3 us
  blocking collectives  26.5 us (87%)
  Pallas kernels  3.73 us (12%)
    all_to_all x2, blocking collectives, exchanged(): lax.all_to_all(x, axis, 0, 0, tiled=True, axis_index_groups=[order_of(axi...  26.5 us
    pallas_call x1, Pallas kernels, per_device(): pl.pallas_call(functools.partial(summary_kernel, total_length), out_shape...  1.79 us
    pallas_call x1, Pallas kernels, per_device(): pl.pallas_call(functools.partial(norm_kernel, channels * lax.axis_size('w...  1.34 us

profile of v3, /device:TPU:1, one launch (start us, length us, event | category | flops | bytes accessed | tf_op | source)
XLA Modules:
  0.0 30.3 jit_solution(7580441424051014224)
XLA Ops:
  0.0 1.8 %summary.1 = (f32[16,8,128]{2,1,0:T(8,128)S(1)}, f32[17,8,128]{2,1,0:T(8,128)S(1)}, f32[256,8,128]{2,1,0:T(8,128)S(1)}, f32[256,8,128]{2,1,0:T(8,128)S(1)}, f32[1,128]{1,0:T(1,128)S(1)}) custom-call(s32[1]{0:T(128)} %bitcast.here_ref, f32[2048,128]{1,0:T(8,128)} %bitcast.5, bf16[2048,128]{1,0:T(8,128)(2,1)} %bitcast.6, f32[1,128]{1,0:T(1,128)} %bitcast.7), custom_call_target="tpu_custom_call" | custom-call | tf_op jit(solution)/shard_map/summary/pallas_call | solution.py:245
  1.8 10.9 %all_to_all.10.all_ends_ref = f32[16,8,128]{2,1,0:T(8,128)S(1)} all-to-all(f32[16,8,128]{2,1,0:T(8,128)S(1)} %get-tuple-element.12), channel_id=1, replica_groups={{160,0,16,32,48,64,80,96,112,128,144,176,192,208,224,240},{161,1,17,33,..., dimensions={0} | all-to-all | bytes 131072 | tf_op jit(solution)/shard_map/all_to_all | solution.py:236
  12.7 0.6 %states.1 = (f32[256,8,128]{2,1,0:T(8,128)S(1)}, f32[16,16,128]{2,1,0:T(8,128)S(1)}) custom-call(f32[16,8,128]{2,1,0:T(8,128)S(1)} %all_to_all.10.all_ends_ref, f32[17,8,128]{2,1,0:T(8,128)S(1)} %get-tuple-element.13.parts_ref, f32[256,8,128]{2,1,0:T(8,128)S(1)} %get-tuple-element.14.keep_ref, f32[256,8,128]{2,1,0:T(8,128)S(1)} %get-tuple-element.15.push_ref), custom_call_target="tpu_custom_call" | custom-call | tf_op jit(solution)/shard_map/states/pallas_call | solution.py:267
  13.3 15.6 %all_to_all.11.all_squares_ref = f32[16,16,128]{2,1,0:T(8,128)S(1)} all-to-all(f32[16,16,128]{2,1,0:T(8,128)S(1)} %get-tuple-element.16), channel_id=1, replica_groups={{9,0,1,2,3,4,5,6,7,8,10,11,12,13,14,15},{25,16,17,18,19,20,21,22,23,24,..., dimensions={0} | all-to-all | bytes 262144 | tf_op jit(solution)/shard_map/all_to_all | solution.py:236
  28.9 1.3 %norm.1 = bf16[2048,128]{1,0:T(8,128)(2,1)} custom-call(f32[16,16,128]{2,1,0:T(8,128)S(1)} %all_to_all.11.all_squares_ref, f32[256,8,128]{2,1,0:T(8,128)S(1)} %get-tuple-element.17.states_ref, f32[1,128]{1,0:T(1,128)S(1)} %get-tuple-element.18.gain_ref), custom_call_target="tpu_custom_call" | custom-call | tf_op jit(solution)/shard_map/norm/pallas_call | solution.py:276

commit v4 on v3

--- a/solution.py
+++ b/solution.py
@@ -15,13 +15,22 @@
 HBM = pl.BlockSpec(memory_space=pltpu.HBM)
 
 
-FIRST = {"seq": 10, "width": 9}
-
-
-def order_of(axis):
-    size = lax.axis_size(axis)
-    first = FIRST[axis] % size
-    return [first] + [member for member in range(size) if member != first]
+FAR_STRETCH = 10
+FAR_CHIP = 4
+CORES = 2
+
+
+def far_first(members, far):
+    return [members[far % len(members)]] + [m for m in members if m != members[far % len(members)]]
+
+
+def stretches():
+    return far_first(list(range(lax.axis_size("seq"))), FAR_STRETCH)
+
+
+def chips_of_each_core():
+    size = lax.axis_size("width")
+    return [far_first(list(range(core, size, CORES)), FAR_CHIP) for core in range(CORES)]
 
 
 def groups_of(rows):
@@ -144,7 +153,7 @@
     row = lax.broadcasted_iota(jnp.int32, (SUB, LANES), 0)
     packed = jnp.where(row == 0, product, jnp.where(row == 1, forward, backward))
     for copy in range(ends_ref.shape[0]):
-        ends_ref[copy] = packed
+        ends_ref[copy] = packed[: ends_ref.shape[1]]
     parts_ref[4 * len(groups)] = zero + here_ref[0].astype(F32)
     gain_load.wait()
 
@@ -201,8 +210,7 @@
     done = all_steps(groups, back, {g: (b, zero) for g, b in enumerate(entering_backward)}, reverse=True)
     for half in (0, 1):
         squares = jnp.where(lane < short, done[half][1], done[half + 2][1])
-        for copy in range(squares_ref.shape[0]):
-            squares_ref[copy, pl.ds(half * SUB, SUB), :] = squares
+        squares_ref[pl.ds(half * SUB, SUB), :] = squares
 
 
 def norm_kernel(channels, all_squares_ref, states_ref, gain_ref, out_hbm, rows_ref, out_ref, sent):
@@ -232,8 +240,8 @@
     return pltpu.CompilerParams(vmem_limit_bytes=12 * 1024 * 1024)
 
 
-def exchanged(x, axis):
-    return lax.all_to_all(x, axis, 0, 0, tiled=True, axis_index_groups=[order_of(axis)])
+def exchanged(x, axis, groups):
+    return lax.all_to_all(x, axis, 0, 0, tiled=True, axis_index_groups=groups)
 
 
 def per_device(leak_rate, signal_in, norm_gain):
@@ -245,7 +253,7 @@
     ends, parts, keep, push, gain = pl.pallas_call(
         functools.partial(summary_kernel, total_length),
         out_shape=(
-            jax.ShapeDtypeStruct((lax.axis_size("seq"), SUB, LANES), F32),
+            jax.ShapeDtypeStruct((lax.axis_size("seq"), 4, LANES), F32),
             jax.ShapeDtypeStruct((17, SUB, LANES), F32),
             blocks,
             blocks,
@@ -263,16 +271,20 @@
         compiler_params=params(),
         name="summary",
     )(here, *(pltpu.with_memory_space_constraint(x, pltpu.HBM) for x in operands))
-    all_ends = exchanged(ends, "seq")
+    all_ends = exchanged(ends, "seq", [stretches()])
     states, squares = pl.pallas_call(
-        functools.partial(states_kernel, order_of("seq")),
-        out_shape=(blocks, jax.ShapeDtypeStruct((lax.axis_size("width"), 2 * SUB, LANES), F32)),
+        functools.partial(states_kernel, stretches()),
+        out_shape=(blocks, jax.ShapeDtypeStruct((2 * SUB, LANES), F32)),
         in_specs=[VMEM] * 4,
         out_specs=(VMEM,) * 2,
         compiler_params=params(),
         name="states",
     )(all_ends, parts, keep, push)
-    all_squares = exchanged(squares, "width")
+    width = lax.axis_size("width")
+    partners = [(member, member ^ 1) for member in range(width)]
+    squares = squares + lax.ppermute(squares, "width", partners)
+    squares = jnp.broadcast_to(squares[None], (width // CORES, *squares.shape))
+    all_squares = exchanged(squares, "width", chips_of_each_core())
     mixed = pl.pallas_call(
         functools.partial(norm_kernel, channels * lax.axis_size("width")),
         out_shape=jax.ShapeDtypeStruct((rows, LANES), jnp.bfloat16),

time: 30.4 us -> 29.3 us (0.964)
  blocking collectives: 26.5 us -> 22.6 us
  starting transfers between devices: 0 us -> 1.97 us
  waiting for transfers between devices: 0 us -> 0.83 us
    all_to_all x2, blocking collectives: 26.5 us -> 22.6 us  [exchanged(): return lax.all_to_all(x, axis, 0, 0, tiled=True, axis_index_groups=groups)]
    ppermute x0 -> x1, starting transfers between devices: none -> 1.97 us  [per_device(): squares = squares + lax.ppermute(squares, 'width', partners)]
    ppermute x0 -> x1, waiting for transfers between devices: none -> 0.83 us  [per_device(): squares = squares + lax.ppermute(squares, 'width', partners)]
  transfers between devices with their start and end apart: 0 -> 1, of which waited for: 0 -> 1; matrix products, arithmetic and copies ran while one was open for 0% -> 0% of each run, Pallas kernels for 0% -> 0%
where the time goes in v4:
time: 29.3 us; the launch traced here: 29.1 us
  blocking collectives  22.6 us (77%)
  Pallas kernels  3.73 us (13%)
  starting transfers between devices  1.97 us (7%)
  waiting for transfers between devices  0.83 us (3%)
    all_to_all x2, blocking collectives, exchanged(): return lax.all_to_all(x, axis, 0, 0, tiled=True, axis_index_groups=groups)  22.6 us
    ppermute x1, starting transfers between devices, per_device(): squares = squares + lax.ppermute(squares, 'width', partners)  1.97 us
    pallas_call x1, Pallas kernels, per_device(): pl.pallas_call(functools.partial(summary_kernel, total_length), out_shape...  1.79 us
    pallas_call x1, Pallas kernels, per_device(): pl.pallas_call(functools.partial(norm_kernel, channels * lax.axis_size('w...  1.33 us
    ppermute x1, waiting for transfers between devices, per_device(): squares = squares + lax.ppermute(squares, 'width', partners)  0.83 us
    pallas_call x1, Pallas kernels, per_device(): pl.pallas_call(functools.partial(states_kernel, stretches()), out_shape=(...  0.61 us
  transfers between devices with their start and end apart: 1, of which 1 were waited for; matrix products, arithmetic and copies ran while one was open for 0% of the time, Pallas kernels for 0%

profile of v4, /device:TPU:1, one launch (start us, length us, event | category | flops | bytes accessed | tf_op | source)
XLA Modules:
  0.0 29.1 jit_solution(644415932554079518)
XLA Ops:
  0.0 1.8 %summary.1 = (f32[16,4,128]{2,1,0:T(4,128)S(1)}, f32[17,8,128]{2,1,0:T(8,128)S(1)}, f32[256,8,128]{2,1,0:T(8,128)S(1)}, f32[256,8,128]{2,1,0:T(8,128)S(1)}, f32[1,128]{1,0:T(1,128)S(1)}) custom-call(s32[1]{0:T(128)} %bitcast.here_ref, f32[2048,128]{1,0:T(8,128)} %bitcast.5, bf16[2048,128]{1,0:T(8,128)(2,1)} %bitcast.6, f32[1,128]{1,0:T(1,128)} %bitcast.7), custom_call_target="tpu_custom_call" | custom-call | tf_op jit(solution)/shard_map/summary/pallas_call | solution.py:253
  1.8 10.8 %all_to_all.10.all_ends_ref = f32[16,4,128]{2,1,0:T(4,128)S(1)} all-to-all(f32[16,4,128]{2,1,0:T(4,128)S(1)} %get-tuple-element.12), channel_id=1, replica_groups={{160,0,16,32,48,64,80,96,112,128,144,176,192,208,224,240},{161,1,17,33,..., dimensions={0} | all-to-all | bytes 65536 | tf_op jit(solution)/shard_map/all_to_all | solution.py:244
  12.6 0.6 %states.1 = (f32[256,8,128]{2,1,0:T(8,128)S(1)}, f32[16,128]{1,0:T(8,128)S(1)}) custom-call(f32[16,4,128]{2,1,0:T(4,128)S(1)} %all_to_all.10.all_ends_ref, f32[17,8,128]{2,1,0:T(8,128)S(1)} %get-tuple-element.13.parts_ref, f32[256,8,128]{2,1,0:T(8,128)S(1)} %get-tuple-element.14.keep_ref, f32[256,8,128]{2,1,0:T(8,128)S(1)} %get-tuple-element.15.push_ref), custom_call_target="tpu_custom_call" | custom-call | tf_op jit(solution)/shard_map/states/pallas_call | solution.py:275
  13.2 2.0 %collective-permute-start = (f32[16,128]{1,0:T(8,128)S(1)}, f32[16,128]{1,0:T(8,128)S(1)}, u32[]{:S(2)}, u32[]{:S(2)}) collective-permute-start(f32[16,128]{1,0:T(8,128)S(1)} %get-tuple-element.16), channel_id=1, source_target_pairs={{0,1},{1,0},{2,3},{3,2},{4,5},{5,4},{6,7},{7,6},{8,9},{9,8},{10,11... | collective-permute-start | bytes 24584 | tf_op jit(solution)/shard_map/ppermute | solution.py:285
  15.2 0.8 %collective-permute-done = f32[16,128]{1,0:T(8,128)S(1)} collective-permute-done((f32[16,128]{1,0:T(8,128)S(1)}, f32[16,128]{1,0:T(8,128)S(1)}, u32[]{:S(2)}, u32[]{:S(2)}) %collective-permute-start) | collective-permute-done | bytes 8224 | tf_op jit(solution)/shard_map/ppermute | solution.py:285
  16.0 11.8 %all_to_all.11.all_squares_ref = f32[8,16,128]{2,1,0:T(8,128)S(1)} all-to-all(f32[8,16,128]{2,1,0:T(8,128)S(1)} %broadcast_in_dim.4), channel_id=1, replica_groups={{8,0,2,4,6,10,12,14},{9,1,3,5,7,11,13,15},{24,16,18,20,22,26,28,30},{25..., dimensions={0} | all-to-all | bytes 131072 | tf_op jit(solution)/shard_map/all_to_all | solution.py:244
  27.8 1.3 %norm.1 = bf16[2048,128]{1,0:T(8,128)(2,1)} custom-call(f32[8,16,128]{2,1,0:T(8,128)S(1)} %all_to_all.11.all_squares_ref, f32[256,8,128]{2,1,0:T(8,128)S(1)} %get-tuple-element.17.states_ref, f32[1,128]{1,0:T(1,128)S(1)} %get-tuple-element.18.gain_ref), custom_call_target="tpu_custom_call" | custom-call | tf_op jit(solution)/shard_map/norm/pallas_call | solution.py:288
  (2 shorter events, 0.0 us)
Async XLA Ops:
  13.2 2.8 %collective-permute-start = (f32[16,128]{1,0:T(8,128)S(1)}, f32[16,128]{1,0:T(8,128)S(1)}, u32[]{:S(2)}, u32[]{:S(2)}) collective-permute-start(f32[16,128]{1,0:T(8,128)S(1)} %get-tuple-element.16), channel_id=1, source_target_pairs={{0,1},{1,0},{2,3},{3,2},{4,5},{5,4},{6,7},{7,6},{8,9},{9,8},{10,11... | collective-permute-start | bytes 24584 | tf_op jit(solution)/shard_map/ppermute | solution.py:285

commit v5 on v4

--- a/solution.py
+++ b/solution.py
@@ -1,4 +1,5 @@
 import functools
+import math
 
 import jax
 import jax.numpy as jnp
@@ -77,9 +78,8 @@
     return state
 
 
-def rows_of(group):
-    first, _, length = group
-    return pl.ds(first, length * SUB)
+def rows_of(groups, cut):
+    return pl.ds(groups[cut[0]][0], sum(groups[g][2] for g in cut) * SUB)
 
 
 def summary_kernel(
@@ -101,23 +101,21 @@
 ):
     groups = groups_of(leak_ref.shape[0])
     scale = total_length ** (-0.5)
-    loads = []
-    for g, group in enumerate(groups):
-        at = rows_of(group)
-        loads.append(
-            (
-                pltpu.make_async_copy(leak_hbm.at[at], leak_ref.at[at], arrived.at[0, g]),
-                pltpu.make_async_copy(signal_hbm.at[at], signal_ref.at[at], arrived.at[1, g]),
-            )
-        )
-        for load in loads[-1]:
-            load.start()
+    exponent = -math.log2(math.e) / total_length
+    halves = ((0, 1), (2, 3))
+    signal_load = pltpu.make_async_copy(signal_hbm, signal_ref, arrived.at[0])
+    signal_load.start()
+    leak_loads = []
+    for half, cut in enumerate(halves):
+        at = rows_of(groups, cut)
+        leak_loads.append(pltpu.make_async_copy(leak_hbm.at[at], leak_ref.at[at], arrived.at[1 + half]))
+        leak_loads[-1].start()
     gain_load = pltpu.make_async_copy(gain_hbm, gain_ref, gain_arrived)
     gain_load.start()
 
     def body(g, step, state):
         product, forward, backward = state
-        keep = jnp.exp(-leak_ref[rows_at(groups[g], step), :] / total_length)
+        keep = jnp.exp2(leak_ref[rows_at(groups[g], step), :] * exponent)
         push = rows_ref[rows_at(groups[g], step), :]
         keep_ref[groups[g][1] + step] = keep
         push_ref[groups[g][1] + step] = push
@@ -125,16 +123,13 @@
 
     zero = jnp.zeros((SUB, LANES), F32)
     state = {}
-    for pair in ((0, 1), (2, 3)):
-        for g in pair:
-            for load in loads[g]:
-                load.wait()
-        for g in pair:
-            first, _, length = groups[g]
-            for row in range(first, first + length * SUB, 16):
-                at = pl.ds(row, 16)
-                rows_ref[at, :] = signal_ref[at, :].astype(F32) * scale
-        state |= all_steps(groups, body, {g: (zero + 1.0, zero, zero) for g in pair})
+    signal_load.wait()
+    for row in range(0, leak_ref.shape[0], 16):
+        at = pl.ds(row, 16)
+        rows_ref[at, :] = signal_ref[at, :].astype(F32) * scale
+    for cut, load in zip(halves, leak_loads):
+        load.wait()
+        state |= all_steps(groups, body, {g: (zero + 1.0, zero, zero) for g in cut})
     ends = []
     for g in range(len(groups)):
         product, forward, backward = state[g]
@@ -220,18 +215,20 @@
     scale = lax.rsqrt(power + 1e-06)
     halves = (scale[:SUB], scale[SUB:])
     gain = jnp.broadcast_to(gain_ref[...], (SUB, LANES))
+    lanes = lax.broadcasted_iota(jnp.int32, (SUB, LANES), 1)
     stores = []
     for g, (first, at, length) in enumerate(groups):
         for step in range(length):
             lane = step + (short if g >= 2 else 0)
-            factor = jnp.broadcast_to(halves[g % 2][:, lane : lane + 1], (SUB, LANES))
+            factor = jnp.sum(jnp.where(lanes == lane, halves[g % 2], 0.0), axis=1, keepdims=True)
             rows_ref[rows_at(groups[g], step), :] = states_ref[at + step] * factor * gain
         for row in range(first, first + length * SUB, 16):
             here = pl.ds(row, 16)
             out_ref[here, :] = rows_ref[here, :].astype(out_ref.dtype)
-        rows = rows_of(groups[g])
-        stores.append(pltpu.make_async_copy(out_ref.at[rows], out_hbm.at[rows], sent.at[g]))
-        stores[-1].start()
+        if g % 2:
+            rows = rows_of(groups, (g - 1, g))
+            stores.append(pltpu.make_async_copy(out_ref.at[rows], out_hbm.at[rows], sent.at[g // 2]))
+            stores[-1].start()
     for store in stores:
         store.wait()
 
@@ -265,7 +262,7 @@
             pltpu.VMEM((rows, LANES), F32),
             pltpu.VMEM((rows, LANES), signal_in.dtype),
             pltpu.VMEM((rows, LANES), F32),
-            pltpu.SemaphoreType.DMA((2, 4)),
+            pltpu.SemaphoreType.DMA((3,)),
             pltpu.SemaphoreType.DMA,
         ],
         compiler_params=params(),
@@ -293,7 +290,7 @@
         scratch_shapes=[
             pltpu.VMEM((rows, LANES), F32),
             pltpu.VMEM((rows, LANES), jnp.bfloat16),
-            pltpu.SemaphoreType.DMA((4,)),
+            pltpu.SemaphoreType.DMA((2,)),
         ],
         compiler_params=params(),
         name="norm",

time: 29.3 us -> 29 us (0.990)
  Pallas kernels: 3.73 us -> 3.38 us
where the time goes in v5:
time: 29 us; the launch traced here: 28.8 us
  blocking collectives  22.6 us (78%)
  Pallas kernels  3.38 us (12%)
  starting transfers between devices  1.97 us (7%)
  waiting for transfers between devices  0.83 us (3%)
    all_to_all x2, blocking collectives, exchanged(): return lax.all_to_all(x, axis, 0, 0, tiled=True, axis_index_groups=groups)  22.6 us
    ppermute x1, starting transfers between devices, per_device(): squares = squares + lax.ppermute(squares, 'width', partners)  1.97 us
    pallas_call x1, Pallas kernels, per_device(): pl.pallas_call(functools.partial(summary_kernel, total_length), out_shape...  1.58 us
    pallas_call x1, Pallas kernels, per_device(): pl.pallas_call(functools.partial(norm_kernel, channels * lax.axis_size('w...  1.19 us
    ppermute x1, waiting for transfers between devices, per_device(): squares = squares + lax.ppermute(squares, 'width', partners)  0.83 us
    pallas_call x1, Pallas kernels, per_device(): pl.pallas_call(functools.partial(states_kernel, stretches()), out_shape=(...  0.61 us
  transfers between devices with their start and end apart: 1, of which 1 were waited for; matrix products, arithmetic and copies ran while one was open for 0% of the time, Pallas kernels for 0%

profile of v5, /device:TPU:1, one launch (start us, length us, event | category | flops | bytes accessed | tf_op | source)
XLA Modules:
  0.0 28.8 jit_solution(2216306916766617837)
XLA Ops:
  0.0 1.6 %summary.1 = (f32[16,4,128]{2,1,0:T(4,128)S(1)}, f32[17,8,128]{2,1,0:T(8,128)S(1)}, f32[256,8,128]{2,1,0:T(8,128)S(1)}, f32[256,8,128]{2,1,0:T(8,128)S(1)}, f32[1,128]{1,0:T(1,128)S(1)}) custom-call(s32[1]{0:T(128)} %bitcast.here_ref, f32[2048,128]{1,0:T(8,128)} %bitcast.5, bf16[2048,128]{1,0:T(8,128)(2,1)} %bitcast.6, f32[1,128]{1,0:T(1,128)} %bitcast.7), custom_call_target="tpu_custom_call" | custom-call | tf_op jit(solution)/shard_map/summary/pallas_call | solution.py:250
  1.6 10.8 %all_to_all.10.all_ends_ref = f32[16,4,128]{2,1,0:T(4,128)S(1)} all-to-all(f32[16,4,128]{2,1,0:T(4,128)S(1)} %get-tuple-element.12), channel_id=1, replica_groups={{160,0,16,32,48,64,80,96,112,128,144,176,192,208,224,240},{161,1,17,33,..., dimensions={0} | all-to-all | bytes 65536 | tf_op jit(solution)/shard_map/all_to_all | solution.py:241
  12.4 0.6 %states.1 = (f32[256,8,128]{2,1,0:T(8,128)S(1)}, f32[16,128]{1,0:T(8,128)S(1)}) custom-call(f32[16,4,128]{2,1,0:T(4,128)S(1)} %all_to_all.10.all_ends_ref, f32[17,8,128]{2,1,0:T(8,128)S(1)} %get-tuple-element.13.parts_ref, f32[256,8,128]{2,1,0:T(8,128)S(1)} %get-tuple-element.14.keep_ref, f32[256,8,128]{2,1,0:T(8,128)S(1)} %get-tuple-element.15.push_ref), custom_call_target="tpu_custom_call" | custom-call | tf_op jit(solution)/shard_map/states/pallas_call | solution.py:272
  13.0 2.0 %collective-permute-start = (f32[16,128]{1,0:T(8,128)S(1)}, f32[16,128]{1,0:T(8,128)S(1)}, u32[]{:S(2)}, u32[]{:S(2)}) collective-permute-start(f32[16,128]{1,0:T(8,128)S(1)} %get-tuple-element.16), channel_id=1, source_target_pairs={{0,1},{1,0},{2,3},{3,2},{4,5},{5,4},{6,7},{7,6},{8,9},{9,8},{10,11... | collective-permute-start | bytes 24584 | tf_op jit(solution)/shard_map/ppermute | solution.py:282
  14.9 0.8 %collective-permute-done = f32[16,128]{1,0:T(8,128)S(1)} collective-permute-done((f32[16,128]{1,0:T(8,128)S(1)}, f32[16,128]{1,0:T(8,128)S(1)}, u32[]{:S(2)}, u32[]{:S(2)}) %collective-permute-start) | collective-permute-done | bytes 8224 | tf_op jit(solution)/shard_map/ppermute | solution.py:282
  15.8 11.8 %all_to_all.11.all_squares_ref = f32[8,16,128]{2,1,0:T(8,128)S(1)} all-to-all(f32[8,16,128]{2,1,0:T(8,128)S(1)} %broadcast_in_dim.4), channel_id=1, replica_groups={{8,0,2,4,6,10,12,14},{9,1,3,5,7,11,13,15},{24,16,18,20,22,26,28,30},{25..., dimensions={0} | all-to-all | bytes 131072 | tf_op jit(solution)/shard_map/all_to_all | solution.py:241
  27.6 1.2 %norm.1 = bf16[2048,128]{1,0:T(8,128)(2,1)} custom-call(f32[8,16,128]{2,1,0:T(8,128)S(1)} %all_to_all.11.all_squares_ref, f32[256,8,128]{2,1,0:T(8,128)S(1)} %get-tuple-element.17.states_ref, f32[1,128]{1,0:T(1,128)S(1)} %get-tuple-element.18.gain_ref), custom_call_target="tpu_custom_call" | custom-call | tf_op jit(solution)/shard_map/norm/pallas_call | solution.py:285
  (2 shorter events, 0.0 us)
Async XLA Ops:
  13.0 2.8 %collective-permute-start = (f32[16,128]{1,0:T(8,128)S(1)}, f32[16,128]{1,0:T(8,128)S(1)}, u32[]{:S(2)}, u32[]{:S(2)}) collective-permute-start(f32[16,128]{1,0:T(8,128)S(1)} %get-tuple-element.16), channel_id=1, source_target_pairs={{0,1},{1,0},{2,3},{3,2},{4,5},{5,4},{6,7},{7,6},{8,9},{9,8},{10,11... | collective-permute-start | bytes 24584 | tf_op jit(solution)/shard_map/ppermute | solution.py:282

commit v6 on v5

--- a/solution.py
+++ b/solution.py
@@ -92,6 +92,8 @@
     parts_ref,
     keep_ref,
     push_ref,
+    product_ref,
+    forward_ref,
     gain_ref,
     leak_ref,
     signal_ref,
@@ -119,7 +121,11 @@
         push = rows_ref[rows_at(groups[g], step), :]
         keep_ref[groups[g][1] + step] = keep
         push_ref[groups[g][1] + step] = push
-        return (product * keep, forward * keep + push, backward + product * push)
+        backward = backward + product * push
+        product, forward = product * keep, forward * keep + push
+        product_ref[groups[g][1] + step] = product
+        forward_ref[groups[g][1] + step] = forward
+        return (product, forward, backward)
 
     zero = jnp.zeros((SUB, LANES), F32)
     state = {}
@@ -153,7 +159,18 @@
     gain_load.wait()
 
 
-def states_kernel(order, all_ends_ref, parts_ref, keep_ref, push_ref, states_ref, squares_ref):
+def states_kernel(
+    order,
+    all_ends_ref,
+    parts_ref,
+    keep_ref,
+    push_ref,
+    product_ref,
+    forward_ref,
+    gain_ref,
+    states_ref,
+    squares_ref,
+):
     groups = groups_of(keep_ref.shape[0] * SUB)
     here = parts_ref[4 * len(groups), 0:1]
     devices = len(order)
@@ -181,13 +198,7 @@
         )
         backward = backwards[:1] + whole[:1] * backward
 
-    def forth(g, step, state):
-        at = groups[g][1] + step
-        state = state * keep_ref[at] + push_ref[at]
-        states_ref[at] = state
-        return state
-
-    all_steps(groups, forth, dict(enumerate(entering_forward)))
+    gain = jnp.broadcast_to(gain_ref[...], (SUB, LANES))
     lane = lax.broadcasted_iota(jnp.int32, (SUB, LANES), 1)
     short = groups[0][2]
 
@@ -195,8 +206,8 @@
         state, sums = state
         at = groups[g][1] + step
         state = state * keep_ref[at] + push_ref[at]
-        both = states_ref[at] + state
-        states_ref[at] = both
+        both = (forward_ref[at] + product_ref[at] * entering_forward[g]) + state
+        states_ref[at] = both * gain
         power = jnp.sum(both * both, axis=1, keepdims=True)
         sums = jnp.where(lane == step + (short if g >= 2 else 0), power, sums)
         return state, sums
@@ -208,20 +219,19 @@
         squares_ref[pl.ds(half * SUB, SUB), :] = squares
 
 
-def norm_kernel(channels, all_squares_ref, states_ref, gain_ref, out_hbm, rows_ref, out_ref, sent):
+def norm_kernel(channels, all_squares_ref, states_ref, out_hbm, rows_ref, out_ref, sent):
     groups = groups_of(rows_ref.shape[0])
     short = groups[0][2]
     power = jnp.sum(all_squares_ref[...], axis=0) / channels
     scale = lax.rsqrt(power + 1e-06)
     halves = (scale[:SUB], scale[SUB:])
-    gain = jnp.broadcast_to(gain_ref[...], (SUB, LANES))
     lanes = lax.broadcasted_iota(jnp.int32, (SUB, LANES), 1)
     stores = []
     for g, (first, at, length) in enumerate(groups):
         for step in range(length):
             lane = step + (short if g >= 2 else 0)
             factor = jnp.sum(jnp.where(lanes == lane, halves[g % 2], 0.0), axis=1, keepdims=True)
-            rows_ref[rows_at(groups[g], step), :] = states_ref[at + step] * factor * gain
+            rows_ref[rows_at(groups[g], step), :] = states_ref[at + step] * factor
         for row in range(first, first + length * SUB, 16):
             here = pl.ds(row, 16)
             out_ref[here, :] = rows_ref[here, :].astype(out_ref.dtype)
@@ -247,17 +257,19 @@
     blocks = jax.ShapeDtypeStruct((rows // SUB, SUB, LANES), F32)
     here = lax.axis_index("seq").astype(jnp.int32).reshape(1)
     operands = (leak_rate[0], signal_in[0], norm_gain.reshape(1, channels))
-    ends, parts, keep, push, gain = pl.pallas_call(
+    ends, *scanned = pl.pallas_call(
         functools.partial(summary_kernel, total_length),
         out_shape=(
             jax.ShapeDtypeStruct((lax.axis_size("seq"), 4, LANES), F32),
             jax.ShapeDtypeStruct((17, SUB, LANES), F32),
             blocks,
             blocks,
+            blocks,
+            blocks,
             jax.ShapeDtypeStruct((1, LANES), F32),
         ),
         in_specs=[SMEM] + [HBM] * 3,
-        out_specs=(VMEM,) * 5,
+        out_specs=(VMEM,) * 7,
         scratch_shapes=[
             pltpu.VMEM((rows, LANES), F32),
             pltpu.VMEM((rows, LANES), signal_in.dtype),
@@ -272,11 +284,11 @@
     states, squares = pl.pallas_call(
         functools.partial(states_kernel, stretches()),
         out_shape=(blocks, jax.ShapeDtypeStruct((2 * SUB, LANES), F32)),
-        in_specs=[VMEM] * 4,
+        in_specs=[VMEM] * 7,
         out_specs=(VMEM,) * 2,
         compiler_params=params(),
         name="states",
-    )(all_ends, parts, keep, push)
+    )(all_ends, *scanned)
     width = lax.axis_size("width")
     partners = [(member, member ^ 1) for member in range(width)]
     squares = squares + lax.ppermute(squares, "width", partners)
@@ -285,7 +297,7 @@
     mixed = pl.pallas_call(
         functools.partial(norm_kernel, channels * lax.axis_size("width")),
         out_shape=jax.ShapeDtypeStruct((rows, LANES), jnp.bfloat16),
-        in_specs=[VMEM] * 3,
+        in_specs=[VMEM] * 2,
         out_specs=HBM,
         scratch_shapes=[
             pltpu.VMEM((rows, LANES), F32),
@@ -294,7 +306,7 @@
         ],
         compiler_params=params(),
         name="norm",
-    )(all_squares, states, gain)
+    )(all_squares, states)
     return mixed[None]
 
 

time: 29 us -> 28.8 us (level)
  no operation moved by 1% of the time
where the time goes in v6:
time: 28.8 us; the launch traced here: 28.6 us
  blocking collectives  22.6 us (78%)
  Pallas kernels  3.24 us (11%)
  starting transfers between devices  1.97 us (7%)
  waiting for transfers between devices  0.83 us (3%)
    all_to_all x2, blocking collectives, exchanged(): return lax.all_to_all(x, axis, 0, 0, tiled=True, axis_index_groups=groups)  22.6 us
    ppermute x1, starting transfers between devices, per_device(): squares = squares + lax.ppermute(squares, 'width', partners)  1.97 us
    pallas_call x1, Pallas kernels, per_device(): pl.pallas_call(functools.partial(summary_kernel, total_length), out_shape...  1.62 us
    pallas_call x1, Pallas kernels, per_device(): pl.pallas_call(functools.partial(norm_kernel, channels * lax.axis_size('w...  1.19 us
    ppermute x1, waiting for transfers between devices, per_device(): squares = squares + lax.ppermute(squares, 'width', partners)  0.83 us
  transfers between devices with their start and end apart: 1, of which 1 were waited for; matrix products, arithmetic and copies ran while one was open for 0% of the time, Pallas kernels for 0%

profile of v6, /device:TPU:1, one launch (start us, length us, event | category | flops | bytes accessed | tf_op | source)
XLA Modules:
  0.0 28.6 jit_solution(11726399728239386069)
XLA Ops:
  0.0 1.6 %summary.1 = (f32[16,4,128]{2,1,0:T(4,128)S(1)}, f32[17,8,128]{2,1,0:T(8,128)S(1)}, f32[256,8,128]{2,1,0:T(8,128)S(1)}, f32[256,8,128]{2,1,0:T(8,128)S(1)}, f32[...) custom-call(s32[1]{0:T(128)} %bitcast.here_ref, f32[2048,128]{1,0:T(8,128)} %bitcast.5, ...), custom_call_target="tpu_custom_call" | custom-call | tf_op jit(solution)/shard_map/summary/pallas_call | solution.py:260
  1.6 10.8 %all_to_all.10.all_ends_ref = f32[16,4,128]{2,1,0:T(4,128)S(1)} all-to-all(f32[16,4,128]{2,1,0:T(4,128)S(1)} %get-tuple-element.14), channel_id=1, replica_groups={{160,0,16,32,48,64,80,96,112,128,144,176,192,208,224,240},{161,1,17,33,..., dimensions={0} | all-to-all | bytes 65536 | tf_op jit(solution)/shard_map/all_to_all | solution.py:251
  12.4 0.4 %states.1 = (f32[256,8,128]{2,1,0:T(8,128)S(1)}, f32[16,128]{1,0:T(8,128)S(1)}) custom-call(f32[16,4,128]{2,1,0:T(4,128)S(1)} %all_to_all.10.all_ends_ref, f32[17,8,128]{2,1,0:T(8,128)S(1)} %get-tuple-element.15.parts_ref, f32[256,8,128]{2,1,0:T(8,128)S(1)} %get-tuple-element.16.keep_ref, f32[256,8,128]{2,1,0:T(8,128)S(1)} %get-tuple-element.17.push_ref, ...), custom_call_target="tpu_custom_call" | custom-call | tf_op jit(solution)/shard_map/states/pallas_call | solution.py:284
  12.8 2.0 %collective-permute-start = (f32[16,128]{1,0:T(8,128)S(1)}, f32[16,128]{1,0:T(8,128)S(1)}, u32[]{:S(2)}, u32[]{:S(2)}) collective-permute-start(f32[16,128]{1,0:T(8,128)S(1)} %get-tuple-element.21), channel_id=1, source_target_pairs={{0,1},{1,0},{2,3},{3,2},{4,5},{5,4},{6,7},{7,6},{8,9},{9,8},{10,11... | collective-permute-start | bytes 24584 | tf_op jit(solution)/shard_map/ppermute | solution.py:294
  14.8 0.8 %collective-permute-done = f32[16,128]{1,0:T(8,128)S(1)} collective-permute-done((f32[16,128]{1,0:T(8,128)S(1)}, f32[16,128]{1,0:T(8,128)S(1)}, u32[]{:S(2)}, u32[]{:S(2)}) %collective-permute-start) | collective-permute-done | bytes 8224 | tf_op jit(solution)/shard_map/ppermute | solution.py:294
  15.6 11.8 %all_to_all.11.all_squares_ref = f32[8,16,128]{2,1,0:T(8,128)S(1)} all-to-all(f32[8,16,128]{2,1,0:T(8,128)S(1)} %broadcast_in_dim.4), channel_id=1, replica_groups={{8,0,2,4,6,10,12,14},{9,1,3,5,7,11,13,15},{24,16,18,20,22,26,28,30},{25..., dimensions={0} | all-to-all | bytes 131072 | tf_op jit(solution)/shard_map/all_to_all | solution.py:251
  27.4 1.2 %norm.1 = bf16[2048,128]{1,0:T(8,128)(2,1)} custom-call(f32[8,16,128]{2,1,0:T(8,128)S(1)} %all_to_all.11.all_squares_ref, f32[256,8,128]{2,1,0:T(8,128)S(1)} %get-tuple-element.22.states_ref), custom_call_target="tpu_custom_call" | custom-call | tf_op jit(solution)/shard_map/norm/pallas_call | solution.py:297
  (2 shorter events, 0.0 us)
Async XLA Ops:
  12.8 2.8 %collective-permute-start = (f32[16,128]{1,0:T(8,128)S(1)}, f32[16,128]{1,0:T(8,128)S(1)}, u32[]{:S(2)}, u32[]{:S(2)}) collective-permute-start(f32[16,128]{1,0:T(8,128)S(1)} %get-tuple-element.21), channel_id=1, source_target_pairs={{0,1},{1,0},{2,3},{3,2},{4,5},{5,4},{6,7},{7,6},{8,9},{9,8},{10,11... | collective-permute-start | bytes 24584 | tf_op jit(solution)/shard_map/ppermute | solution.py:294

commit v7 on v6

--- a/solution.py
+++ b/solution.py
@@ -39,7 +39,7 @@
     short = steps // 4 - 4
     assert rows % SUB == 0 and short % 8 == 4 and short + 68 <= LANES
     cuts, at = [], 0
-    for length in (short, short, short + 8, short + 8):
+    for length in (short + 8, short + 8, short, short):
         cuts.append((at * SUB, at, length))
         at += length
     assert at == steps
@@ -128,24 +128,23 @@
         return (product, forward, backward)
 
     zero = jnp.zeros((SUB, LANES), F32)
-    state = {}
+    ends = []
     signal_load.wait()
     for row in range(0, leak_ref.shape[0], 16):
         at = pl.ds(row, 16)
         rows_ref[at, :] = signal_ref[at, :].astype(F32) * scale
     for cut, load in zip(halves, leak_loads):
         load.wait()
-        state |= all_steps(groups, body, {g: (zero + 1.0, zero, zero) for g in cut})
-    ends = []
-    for g in range(len(groups)):
-        product, forward, backward = state[g]
-        whole, forwards = scan_sublanes(product, forward, earlier_sublanes)
-        turned, backwards = scan_sublanes(product, backward, later_sublanes)
-        parts_ref[4 * g] = whole
-        parts_ref[4 * g + 1] = forwards
-        parts_ref[4 * g + 2] = turned
-        parts_ref[4 * g + 3] = backwards
-        ends.append((whole[SUB - 1 :], forwards[SUB - 1 :], backwards[:1]))
+        state = all_steps(groups, body, {g: (zero + 1.0, zero, zero) for g in cut})
+        for g in cut:
+            product, forward, backward = state[g]
+            whole, forwards = scan_sublanes(product, forward, earlier_sublanes)
+            turned, backwards = scan_sublanes(product, backward, later_sublanes)
+            parts_ref[4 * g] = whole
+            parts_ref[4 * g + 1] = forwards
+            parts_ref[4 * g + 2] = turned
+            parts_ref[4 * g + 3] = backwards
+            ends.append((whole[SUB - 1 :], forwards[SUB - 1 :], backwards[:1]))
     product, forward, backward = ends[0][0], ends[0][1], ends[-1][2]
     for whole, forwards, _ in ends[1:]:
         product, forward = product * whole, forward * whole + forwards
@@ -157,6 +156,15 @@
         ends_ref[copy] = packed[: ends_ref.shape[1]]
     parts_ref[4 * len(groups)] = zero + here_ref[0].astype(F32)
     gain_load.wait()
+
+
+def joined(pieces):
+    while len(pieces) > 1:
+        pieces = [
+            (first[0] * second[0], first[1] * second[0] + second[1])
+            for first, second in zip(pieces[::2], pieces[1::2])
+        ]
+    return pieces[0]
 
 
 def states_kernel(
@@ -175,14 +183,18 @@
     here = parts_ref[4 * len(groups), 0:1]
     devices = len(order)
     place = [order.index(d) for d in range(devices)]
-    forward = jnp.zeros((1, LANES), F32)
-    backward = jnp.zeros((1, LANES), F32)
+    earlier, later = [], []
     for d in range(devices):
-        joined = forward * all_ends_ref[place[d], 0:1] + all_ends_ref[place[d], 1:2]
-        forward = jnp.where(d < here, joined, forward)
-        e = devices - 1 - d
-        joined = backward * all_ends_ref[place[e], 0:1] + all_ends_ref[place[e], 2:3]
-        backward = jnp.where(e > here, joined, backward)
+        product = all_ends_ref[place[d], 0:1]
+        before, after = d < here, d > here
+        earlier.append(
+            (jnp.where(before, product, 1.0), jnp.where(before, all_ends_ref[place[d], 1:2], 0.0))
+        )
+        later.append(
+            (jnp.where(after, product, 1.0), jnp.where(after, all_ends_ref[place[d], 2:3], 0.0))
+        )
+    forward = joined(earlier)[1]
+    backward = joined(later[::-1])[1]
 
     entering_forward, entering_backward = [], [None] * len(groups)
     for g in range(len(groups)):

time: 28.8 us -> 28.8 us (level)
  no operation moved by 1% of the time
where the time goes in v7:
time: 28.8 us; the launch traced here: 28.6 us
  blocking collectives  22.6 us (78%)
  Pallas kernels  3.21 us (11%)
  starting transfers between devices  1.97 us (7%)
  waiting for transfers between devices  0.83 us (3%)
    all_to_all x2, blocking collectives, exchanged(): return lax.all_to_all(x, axis, 0, 0, tiled=True, axis_index_groups=groups)  22.6 us
    ppermute x1, starting transfers between devices, per_device(): squares = squares + lax.ppermute(squares, 'width', partners)  1.97 us
    pallas_call x1, Pallas kernels, per_device(): pl.pallas_call(functools.partial(summary_kernel, total_length), out_shape...  1.62 us
    pallas_call x1, Pallas kernels, per_device(): pl.pallas_call(functools.partial(norm_kernel, channels * lax.axis_size('w...  1.17 us
    ppermute x1, waiting for transfers between devices, per_device(): squares = squares + lax.ppermute(squares, 'width', partners)  0.83 us
  transfers between devices with their start and end apart: 1, of which 1 were waited for; matrix products, arithmetic and copies ran while one was open for 0% of the time, Pallas kernels for 0%

profile of v7, /device:TPU:1, one launch (start us, length us, event | category | flops | bytes accessed | tf_op | source)
XLA Modules:
  0.0 28.6 jit_solution(3480042134733327319)
XLA Ops:
  0.0 1.6 %summary.1 = (f32[16,4,128]{2,1,0:T(4,128)S(1)}, f32[17,8,128]{2,1,0:T(8,128)S(1)}, f32[256,8,128]{2,1,0:T(8,128)S(1)}, f32[256,8,128]{2,1,0:T(8,128)S(1)}, f32[...) custom-call(s32[1]{0:T(128)} %bitcast.here_ref, f32[2048,128]{1,0:T(8,128)} %bitcast.5, ...), custom_call_target="tpu_custom_call" | custom-call | tf_op jit(solution)/shard_map/summary/pallas_call | solution.py:272
  1.6 10.8 %all_to_all.10.all_ends_ref = f32[16,4,128]{2,1,0:T(4,128)S(1)} all-to-all(f32[16,4,128]{2,1,0:T(4,128)S(1)} %get-tuple-element.14), channel_id=1, replica_groups={{160,0,16,32,48,64,80,96,112,128,144,176,192,208,224,240},{161,1,17,33,..., dimensions={0} | all-to-all | bytes 65536 | tf_op jit(solution)/shard_map/all_to_all | solution.py:263
  12.4 0.4 %states.1 = (f32[256,8,128]{2,1,0:T(8,128)S(1)}, f32[16,128]{1,0:T(8,128)S(1)}) custom-call(f32[16,4,128]{2,1,0:T(4,128)S(1)} %all_to_all.10.all_ends_ref, f32[17,8,128]{2,1,0:T(8,128)S(1)} %get-tuple-element.15.parts_ref, f32[256,8,128]{2,1,0:T(8,128)S(1)} %get-tuple-element.16.keep_ref, f32[256,8,128]{2,1,0:T(8,128)S(1)} %get-tuple-element.17.push_ref, ...), custom_call_target="tpu_custom_call" | custom-call | tf_op jit(solution)/shard_map/states/pallas_call | solution.py:296
  12.8 2.0 %collective-permute-start = (f32[16,128]{1,0:T(8,128)S(1)}, f32[16,128]{1,0:T(8,128)S(1)}, u32[]{:S(2)}, u32[]{:S(2)}) collective-permute-start(f32[16,128]{1,0:T(8,128)S(1)} %get-tuple-element.21), channel_id=1, source_target_pairs={{0,1},{1,0},{2,3},{3,2},{4,5},{5,4},{6,7},{7,6},{8,9},{9,8},{10,11... | collective-permute-start | bytes 24584 | tf_op jit(solution)/shard_map/ppermute | solution.py:306
  14.8 0.8 %collective-permute-done = f32[16,128]{1,0:T(8,128)S(1)} collective-permute-done((f32[16,128]{1,0:T(8,128)S(1)}, f32[16,128]{1,0:T(8,128)S(1)}, u32[]{:S(2)}, u32[]{:S(2)}) %collective-permute-start) | collective-permute-done | bytes 8224 | tf_op jit(solution)/shard_map/ppermute | solution.py:306
  15.6 11.8 %all_to_all.11.all_squares_ref = f32[8,16,128]{2,1,0:T(8,128)S(1)} all-to-all(f32[8,16,128]{2,1,0:T(8,128)S(1)} %broadcast_in_dim.4), channel_id=1, replica_groups={{8,0,2,4,6,10,12,14},{9,1,3,5,7,11,13,15},{24,16,18,20,22,26,28,30},{25..., dimensions={0} | all-to-all | bytes 131072 | tf_op jit(solution)/shard_map/all_to_all | solution.py:263
  27.4 1.2 %norm.1 = bf16[2048,128]{1,0:T(8,128)(2,1)} custom-call(f32[8,16,128]{2,1,0:T(8,128)S(1)} %all_to_all.11.all_squares_ref, f32[256,8,128]{2,1,0:T(8,128)S(1)} %get-tuple-element.22.states_ref), custom_call_target="tpu_custom_call" | custom-call | tf_op jit(solution)/shard_map/norm/pallas_call | solution.py:309
  (2 shorter events, 0.0 us)
Async XLA Ops:
  12.8 2.8 %collective-permute-start = (f32[16,128]{1,0:T(8,128)S(1)}, f32[16,128]{1,0:T(8,128)S(1)}, u32[]{:S(2)}, u32[]{:S(2)}) collective-permute-start(f32[16,128]{1,0:T(8,128)S(1)} %get-tuple-element.21), channel_id=1, source_target_pairs={{0,1},{1,0},{2,3},{3,2},{4,5},{5,4},{6,7},{7,6},{8,9},{9,8},{10,11... | collective-permute-start | bytes 24584 | tf_op jit(solution)/shard_map/ppermute | solution.py:306

commit v8 on v7

--- a/solution.py
+++ b/solution.py
@@ -39,7 +39,7 @@
     short = steps // 4 - 4
     assert rows % SUB == 0 and short % 8 == 4 and short + 68 <= LANES
     cuts, at = [], 0
-    for length in (short + 8, short + 8, short, short):
+    for length in (short, short, short + 8, short + 8):
         cuts.append((at * SUB, at, length))
         at += length
     assert at == steps
@@ -128,23 +128,24 @@
         return (product, forward, backward)
 
     zero = jnp.zeros((SUB, LANES), F32)
-    ends = []
+    state = {}
     signal_load.wait()
     for row in range(0, leak_ref.shape[0], 16):
         at = pl.ds(row, 16)
         rows_ref[at, :] = signal_ref[at, :].astype(F32) * scale
     for cut, load in zip(halves, leak_loads):
         load.wait()
-        state = all_steps(groups, body, {g: (zero + 1.0, zero, zero) for g in cut})
-        for g in cut:
-            product, forward, backward = state[g]
-            whole, forwards = scan_sublanes(product, forward, earlier_sublanes)
-            turned, backwards = scan_sublanes(product, backward, later_sublanes)
-            parts_ref[4 * g] = whole
-            parts_ref[4 * g + 1] = forwards
-            parts_ref[4 * g + 2] = turned
-            parts_ref[4 * g + 3] = backwards
-            ends.append((whole[SUB - 1 :], forwards[SUB - 1 :], backwards[:1]))
+        state |= all_steps(groups, body, {g: (zero + 1.0, zero, zero) for g in cut})
+    ends = []
+    for g in range(len(groups)):
+        product, forward, backward = state[g]
+        whole, forwards = scan_sublanes(product, forward, earlier_sublanes)
+        turned, backwards = scan_sublanes(product, backward, later_sublanes)
+        parts_ref[4 * g] = whole
+        parts_ref[4 * g + 1] = forwards
+        parts_ref[4 * g + 2] = turned
+        parts_ref[4 * g + 3] = backwards
+        ends.append((whole[SUB - 1 :], forwards[SUB - 1 :], backwards[:1]))
     product, forward, backward = ends[0][0], ends[0][1], ends[-1][2]
     for whole, forwards, _ in ends[1:]:
         product, forward = product * whole, forward * whole + forwards

time: 28.8 us -> 28.8 us (level)
  no operation moved by 1% of the time
where the time goes in v8:
time: 28.8 us; the launch traced here: 28.6 us
  blocking collectives  22.6 us (78%)
  Pallas kernels  3.22 us (11%)
  starting transfers between devices  1.97 us (7%)
  waiting for transfers between devices  0.83 us (3%)
    all_to_all x2, blocking collectives, exchanged(): return lax.all_to_all(x, axis, 0, 0, tiled=True, axis_index_groups=groups)  22.6 us
    ppermute x1, starting transfers between devices, per_device(): squares = squares + lax.ppermute(squares, 'width', partners)  1.97 us
    pallas_call x1, Pallas kernels, per_device(): pl.pallas_call(functools.partial(summary_kernel, total_length), out_shape...  1.62 us
    pallas_call x1, Pallas kernels, per_device(): pl.pallas_call(functools.partial(norm_kernel, channels * lax.axis_size('w...  1.19 us
    ppermute x1, waiting for transfers between devices, per_device(): squares = squares + lax.ppermute(squares, 'width', partners)  0.83 us
  transfers between devices with their start and end apart: 1, of which 1 were waited for; matrix products, arithmetic and copies ran while one was open for 0% of the time, Pallas kernels for 0%

profile of v8, /device:TPU:1, one launch (start us, length us, event | category | flops | bytes accessed | tf_op | source)
XLA Modules:
  0.0 28.6 jit_solution(9390248950500851138)
XLA Ops:
  0.0 1.6 %summary.1 = (f32[16,4,128]{2,1,0:T(4,128)S(1)}, f32[17,8,128]{2,1,0:T(8,128)S(1)}, f32[256,8,128]{2,1,0:T(8,128)S(1)}, f32[256,8,128]{2,1,0:T(8,128)S(1)}, f32[...) custom-call(s32[1]{0:T(128)} %bitcast.here_ref, f32[2048,128]{1,0:T(8,128)} %bitcast.5, ...), custom_call_target="tpu_custom_call" | custom-call | tf_op jit(solution)/shard_map/summary/pallas_call | solution.py:273
  1.6 10.8 %all_to_all.10.all_ends_ref = f32[16,4,128]{2,1,0:T(4,128)S(1)} all-to-all(f32[16,4,128]{2,1,0:T(4,128)S(1)} %get-tuple-element.14), channel_id=1, replica_groups={{160,0,16,32,48,64,80,96,112,128,144,176,192,208,224,240},{161,1,17,33,..., dimensions={0} | all-to-all | bytes 65536 | tf_op jit(solution)/shard_map/all_to_all | solution.py:264
  12.4 0.4 %states.1 = (f32[256,8,128]{2,1,0:T(8,128)S(1)}, f32[16,128]{1,0:T(8,128)S(1)}) custom-call(f32[16,4,128]{2,1,0:T(4,128)S(1)} %all_to_all.10.all_ends_ref, f32[17,8,128]{2,1,0:T(8,128)S(1)} %get-tuple-element.15.parts_ref, f32[256,8,128]{2,1,0:T(8,128)S(1)} %get-tuple-element.16.keep_ref, f32[256,8,128]{2,1,0:T(8,128)S(1)} %get-tuple-element.17.push_ref, ...), custom_call_target="tpu_custom_call" | custom-call | tf_op jit(solution)/shard_map/states/pallas_call | solution.py:297
  12.8 2.0 %collective-permute-start = (f32[16,128]{1,0:T(8,128)S(1)}, f32[16,128]{1,0:T(8,128)S(1)}, u32[]{:S(2)}, u32[]{:S(2)}) collective-permute-start(f32[16,128]{1,0:T(8,128)S(1)} %get-tuple-element.21), channel_id=1, source_target_pairs={{0,1},{1,0},{2,3},{3,2},{4,5},{5,4},{6,7},{7,6},{8,9},{9,8},{10,11... | collective-permute-start | bytes 24584 | tf_op jit(solution)/shard_map/ppermute | solution.py:307
  14.8 0.8 %collective-permute-done = f32[16,128]{1,0:T(8,128)S(1)} collective-permute-done((f32[16,128]{1,0:T(8,128)S(1)}, f32[16,128]{1,0:T(8,128)S(1)}, u32[]{:S(2)}, u32[]{:S(2)}) %collective-permute-start) | collective-permute-done | bytes 8224 | tf_op jit(solution)/shard_map/ppermute | solution.py:307
  15.6 11.8 %all_to_all.11.all_squares_ref = f32[8,16,128]{2,1,0:T(8,128)S(1)} all-to-all(f32[8,16,128]{2,1,0:T(8,128)S(1)} %broadcast_in_dim.4), channel_id=1, replica_groups={{8,0,2,4,6,10,12,14},{9,1,3,5,7,11,13,15},{24,16,18,20,22,26,28,30},{25..., dimensions={0} | all-to-all | bytes 131072 | tf_op jit(solution)/shard_map/all_to_all | solution.py:264
  27.4 1.2 %norm.1 = bf16[2048,128]{1,0:T(8,128)(2,1)} custom-call(f32[8,16,128]{2,1,0:T(8,128)S(1)} %all_to_all.11.all_squares_ref, f32[256,8,128]{2,1,0:T(8,128)S(1)} %get-tuple-element.22.states_ref), custom_call_target="tpu_custom_call" | custom-call | tf_op jit(solution)/shard_map/norm/pallas_call | solution.py:310
  (2 shorter events, 0.0 us)
Async XLA Ops:
  12.8 2.8 %collective-permute-start = (f32[16,128]{1,0:T(8,128)S(1)}, f32[16,128]{1,0:T(8,128)S(1)}, u32[]{:S(2)}, u32[]{:S(2)}) collective-permute-start(f32[16,128]{1,0:T(8,128)S(1)} %get-tuple-element.21), channel_id=1, source_target_pairs={{0,1},{1,0},{2,3},{3,2},{4,5},{5,4},{6,7},{7,6},{8,9},{9,8},{10,11... | collective-permute-start | bytes 24584 | tf_op jit(solution)/shard_map/ppermute | solution.py:307
